TPU v7x, 512 devices: a whole 4x4x16 slice. The times are simulated.
512 devices in a mesh: seq: 32 (over z, core), head: 16 (over y, x).
Axes of the slice: x: 4, y: 4, z: 16, core: 2. Of those that a mesh axis runs over, the one named last changes fastest.
Arguments:
- queries: bfloat16 [65536, 16, 128], P(('seq', 'head')), may hold values from -6 to 6
- keys: bfloat16 [65536, 16, 128], P(('seq', 'head')), may hold values from -6 to 6
- values: bfloat16 [65536, 16, 128], P(('seq', 'head')), may hold values from -6 to 6
- beta: float32 [65536, 16], P(('seq', 'head')), may hold values from 0 to 1
- log_decay: float32 [65536, 16], P(('seq', 'head')), may hold values from -1 to 0
- out_gate: bfloat16 [65536, 16, 128], P(('seq', 'head')), may hold values from -6 to 6
- norm_gain: float32 [128], replicated, may hold values from 0.1 to 1.9
Outputs:
- gated_out: bfloat16 [65536, 16, 128], P('seq', 'head')
All inputs are finite; a program needn't handle non-finite values.
Results may differ from a plain program's by a relative error of at most 0.001.
Values may be sent and summed in bfloat16 or wider, within the bound.
No kernel may reach another device: no remote copies, remote signals or barrier semaphores. Data moves between devices by JAX's collectives and lax.ppermute only.
A program may use at most 64 MiB of HBM per device.

v0:
```python
import jax
import jax.numpy as jnp
from jax import lax
from jax.experimental import pallas as pl
from jax.experimental.pallas import tpu as pltpu
from jax.sharding import Mesh
from jax.sharding import PartitionSpec as P


F32 = jnp.float32
BF16 = jnp.bfloat16
N = 128
EPS = 1e-06
SUB = 16


def dot(a, b):
    return jnp.dot(a, b, preferred_element_type=F32)


def dot_nt(a, b):
    return lax.dot_general(a, b, (((1,), (1,)), ((), ())), preferred_element_type=F32)


def split2(x):
    high = x.astype(BF16)
    return high, (x - high.astype(F32)).astype(BF16)


def lanes(*parts):
    return jnp.concatenate(parts, axis=1)


def rows(*parts):
    return jnp.concatenate(parts, axis=0)


def square_mm(a_parts, b_parts):
    b_both = lanes(*b_parts)
    both = dot(lanes(*a_parts), rows(b_both, b_both))
    return both[:, :N] + both[:, N:]


def wide_mm(a_parts, b_high, b_low):
    return dot(lanes(*a_parts), rows(b_high, b_high)) + dot(a_parts[0], b_low)


def compose(later, earlier):
    high, low = split2(earlier)
    out = wide_mm(split2(later[:, :N]), high, low)
    return out + lanes(jnp.zeros((N, N), F32), later[:, N:])


def iotas():
    return lax.broadcasted_iota(jnp.int32, (N, N), 0), lax.broadcasted_iota(jnp.int32, (N, N), 1)


def pack_kernel(k_hbm, v_hbm, beta_hbm, decay_hbm, out_ref, k_ref, v_ref, beta_ref, decay_ref, sems):
    heads, tokens = out_ref.shape[0], k_ref.shape[0] // out_ref.shape[0]
    span = N * 2 // heads
    quarter = k_ref.shape[0] // 4
    copies = []
    for i in range(4):
        part = pl.ds(quarter * i, quarter)
        for j, (source, target) in enumerate(((k_hbm, k_ref), (v_hbm, v_ref))):
            copies.append(
                pltpu.make_async_copy(source.at[part], target.at[part], sems.at[2 * i + j])
            )
            copies[-1].start()
    for i, (source, target) in enumerate(((beta_hbm, beta_ref), (decay_hbm, decay_ref))):
        copies.append(pltpu.make_async_copy(source, target, sems.at[8 + i]))
        copies[-1].start()
    shape2 = (2 * N, 2 * N)
    r = lax.broadcasted_iota(jnp.int32, shape2, 0)
    c = lax.broadcasted_iota(jnp.int32, shape2, 1)
    order = (c == r % span * heads + r // span).astype(F32).astype(BF16)
    for i in range(tokens // span):
        part = pl.ds(2 * N * i, 2 * N)
        if 2 * N * i % quarter == 0:
            copies[2 * N * i // quarter * 2].wait()
            copies[2 * N * i // quarter * 2 + 1].wait()
        moved = dot(order, lanes(k_ref[part, :], v_ref[part, :])).astype(BF16)
        for h in range(heads):
            out_ref[h, span * i : span * (i + 1), :] = moved[span * h : span * (h + 1), :]
    copies[8].wait()
    copies[9].wait()
    both = lanes(decay_ref[...], beta_ref[...])
    high = both.astype(BF16).astype(F32)
    low = both - high
    row = lax.broadcasted_iota(jnp.int32, (8, 2 * N), 0)
    for h in range(heads):
        aux = jnp.where(row == 0, high[h : h + 1, :], jnp.where(row == 1, low[h : h + 1, :], 0.0))
        out_ref[h, tokens : tokens + 8, :] = aux.astype(BF16)


def terms_kernel(kv_ref, total_ref, *rest):
    outs, (en_ref, wu_hi_ref, wu_lo_ref, grow_ref, node_ref), sems = rest[:5], rest[5:10], rest[10]
    blocks = kv_ref.shape[0]
    copies = []

    def save(which, first=0, count=blocks):
        part = pl.ds(first, count)
        copies.append(
            pltpu.make_async_copy(rest[5 + which].at[part], outs[which].at[part], sems.at[len(copies)])
        )
        copies[-1].start()

    r, c = iotas()
    one = lambda cond: cond.astype(F32).astype(BF16)
    lower = one(r >= c)
    eye = (r == c).astype(F32)
    inclusive = r >= c
    strict = r > c
    picks = lanes(one(strict), jnp.ones((N, N), BF16))
    picks = rows(picks, picks)
    lane16 = lax.broadcasted_iota(jnp.int32, (SUB, N), 1)
    row16 = lax.broadcasted_iota(jnp.int32, (SUB, N), 0)
    start16 = (row16 == lane16 % SUB).astype(F32)
    base16 = lane16 // SUB * SUB
    merge_masks = [one((r // m == c // m + 1) & (c // m % 2 == 0)) for m in (16, 32, 64)]
    group = range(blocks)

    keys = [kv_ref[b, :N, :N] for b in group]
    kk = [dot_nt(k, k) for k in keys]
    aux = [kv_ref[b, N : N + 8, :] for b in group]
    summed = [dot(lanes(lower * a[0:1, :N], lower * a[1:2, :N]), picks) for a in aux]
    cum = [s[:, N:] for s in summed]
    beta_row = []
    grow_row = []
    nk_row = []
    nk_col = []
    low = []
    for b in group:
        a = aux[b].astype(F32)
        beta_row.append(a[0:1, N:] + a[1:2, N:])
        grow_row.append(jnp.exp(jnp.sum(eye * cum[b], axis=0, keepdims=True)))
        diag = eye * kk[b]
        nk_row.append(lax.rsqrt(jnp.sum(diag, axis=0, keepdims=True) + EPS))
        nk_col.append(lax.rsqrt(jnp.sum(diag, axis=1, keepdims=True) + EPS))
        beta_col = jnp.sum(eye * beta_row[b], axis=1, keepdims=True)
        fade_n = jnp.exp(summed[b][:, :N]) * nk_row[b]
        en_ref[b] = jnp.where(inclusive, fade_n, 0.0)
        low.append(jnp.where(strict, fade_n * (kk[b] * (beta_col * nk_col[b])), 0.0))
        grow_ref[b] = jnp.broadcast_to(grow_row[b], (8, N))
    save(0)
    save(3)
    inv = []
    for b in group:
        small = sum(
            jnp.where(lane16 // SUB == s, low[b][SUB * s : SUB * (s + 1)], 0.0) for s in range(N // SUB)
        )
        x = start16
        for j in range(SUB - 1):
            col = jnp.take_along_axis(small, base16 + j, axis=1)
            x = x - col * x[j : j + 1, :]
        inv.append(rows(*[jnp.where(lane16 // SUB == s, x, 0.0) for s in range(N // SUB)]))
    low_parts = [split2(x) for x in low]
    for mask in merge_masks:
        parts = [split2(x) for x in inv]
        left = [square_mm(parts[b], [p * mask for p in low_parts[b]]) for b in group]
        left = [split2(x) for x in left]
        inv = [inv[b] - square_mm(left[b], parts[b]) for b in group]
    for_u = [inv[b] * beta_row[b] for b in group]
    for_w = [split2(for_u[b] * (grow_row[b] * nk_row[b])) for b in group]
    for_u = [split2(x) for x in for_u]
    w = [dot(lanes(*for_w[b]), rows(keys[b], keys[b])) for b in group]
    values = [kv_ref[b, :N, N:] for b in group]
    u = [dot(lanes(*for_u[b]), rows(values[b], values[b])) for b in group]
    wu = [lanes(w[b], u[b]) for b in group]
    for b in group:
        wu_hi_ref[b], wu_lo_ref[b] = split2(wu[b])
    save(1)
    save(2)
    last = [x[N - 1 : N, :] for x in cum]
    tail = [jnp.exp(last[b] - cum[b]) * nk_col[b] for b in group]
    faded = [split2(wu[b] * lanes(tail[b], tail[b])) for b in group]
    key_t = [k.T for k in keys]
    out = [dot(lanes(key_t[b], key_t[b]), rows(*faded[b])) for b in group]
    pairs = [lanes(eye * jnp.exp(last[b]) - out[b][:, :N], out[b][:, N:]) for b in group]
    spot = 0
    while len(pairs) > 1:
        for i in range(0, len(pairs), 2):
            node_ref[spot + i // 2] = pairs[i]
        save(4, spot, len(pairs) // 2)
        spot += len(pairs) // 2
        pairs = [compose(pairs[i + 1], pairs[i]) for i in range(0, len(pairs), 2)]
    total_ref[...] = pairs[0]
    for copy in copies:
        copy.wait()


def reach_kernel(kv_ref, qg_ref, gain_ref, *rest):
    sources, (r0_ref, hi_ref, lo_ref, gate_ref) = rest[:5], rest[5:9]
    buffers, sems = rest[9:14], rest[14]
    blocks = kv_ref.shape[0]
    copies = [
        pltpu.make_async_copy(sources[i], buffers[i], sems.at[i]) for i in range(len(sources))
    ]
    for copy in copies:
        copy.start()
    en_ref, wu_hi_ref, wu_lo_ref, grow_ref, node_ref = buffers
    r, c = iotas()
    eye = (r == c).astype(F32)
    for b in range(blocks):
        gate = qg_ref[b, :, N:].astype(F32)
        gate_ref[b] = gate / (1.0 + jnp.exp(-gate)) * gain_ref[...]
    copies[0].wait()
    mixing = [
        split2(en_ref[b] * dot_nt(qg_ref[b, :, :N], kv_ref[b, :N, :N])) for b in range(blocks)
    ]
    copies[1].wait()
    copies[2].wait()
    mixed = [wide_mm(mixing[b], wu_hi_ref[b], wu_lo_ref[b]) for b in range(blocks)]
    copies[3].wait()
    copies[4].wait()
    carried = {}
    base, width = {1: 0}, 1
    while width * 2 < blocks:
        base[width * 2] = base[width] + blocks // width // 2
        width *= 2
    step = blocks // 2
    while step:
        for b in range(step, blocks, 2 * step):
            node = node_ref[base[step] + (b - step) // step // 2]
            carried[b] = compose(node, carried[b - step]) if b > step else node
        step //= 2
    for b in range(blocks):
        q32 = qg_ref[b, :, :N].astype(F32)
        scale = lax.rsqrt(jnp.sum(q32 * q32, axis=1, keepdims=True) + EPS) * N**-0.5
        grow_col = jnp.sum(eye * grow_ref[b, 0:1, :], axis=1, keepdims=True)
        reach = grow_col * q32 - mixed[b][:, :N]
        local = mixed[b][:, N:]
        if b:
            high, low = split2(carried[b])
            out = wide_mm(split2(reach), high, low)
            reach, local = out[:, :N], local + out[:, N:]
        r0_ref[b] = local * scale
        hi_ref[b], lo_ref[b] = split2(reach * scale)


def advance(left, right, extra):
    return square_mm(split2(left), split2(right)) + extra


def pair_kernel(core_ref, own_ref, got_ref, out_ref):
    first = core_ref[0] == 0
    own = own_ref[:, :N]
    left = jnp.where(first, got_ref[:, :N], own)
    right = jnp.where(first, own, got_ref[:, N:])
    out_ref[...] = advance(left, right, jnp.where(first, 0.0, own_ref[:, N:]))


def join_kernel(core_ref, near_ref, map_ref, far_ref, out_ref):
    first = core_ref[0] == 0
    near = near_ref[...]
    left = jnp.where(first, near, map_ref[...])
    out_ref[...] = advance(left, far_ref[...], jnp.where(first, 0.0, near))


def finish_kernel(core_ref, r0_ref, hi_ref, lo_ref, own_ref, swap_ref, first_ref, gate_ref, *rest):
    *far_refs, out_ref = rest
    first = core_ref[0] == 0
    own = own_ref[...]
    swap = swap_ref[...]
    state = advance(
        jnp.where(first, own, swap), sum(ref[...] for ref in far_refs), jnp.where(first, swap, own)
    )
    state = jnp.where(first, state, advance(first_ref[:, :N], state, first_ref[:, N:]))
    y_both = lanes(*split2(state))
    y_both = rows(y_both, y_both)
    for b in range(r0_ref.shape[0]):
        both = dot(lanes(hi_ref[b], lo_ref[b]), y_both)
        res = r0_ref[b] + both[:, :N] + both[:, N:]
        norm = lax.rsqrt(jnp.mean(res * res, axis=1, keepdims=True) + EPS)
        out_ref[b] = (res * norm * gate_ref[b]).astype(BF16)


def call(kernel, out_shape, inputs, core=None, remote=(), spill=(), sems=0):
    vmem = pl.BlockSpec(memory_space=pltpu.VMEM)
    hbm = pl.BlockSpec(memory_space=pltpu.HBM)
    specs = [vmem] * len(inputs) + [hbm] * len(remote)
    inputs = [*inputs, *(pltpu.with_memory_space_constraint(a, pltpu.HBM) for a in remote)]
    if core is not None:
        specs = [pl.BlockSpec(memory_space=pltpu.SMEM)] + specs
        inputs = [core, *inputs]
    return pl.pallas_call(
        kernel,
        out_shape=[*out_shape, *(pltpu.HBM(o.shape, o.dtype) for o in spill)],
        in_specs=specs,
        out_specs=[vmem] * len(out_shape) + [hbm] * len(spill),
        scratch_shapes=[pltpu.VMEM(o.shape, o.dtype) for o in (*remote, *spill)]
        + ([pltpu.SemaphoreType.DMA((sems,))] if sems else []),
        compiler_params=pltpu.CompilerParams(vmem_limit_bytes=40 * 2**20),
    )(*inputs)


def near(*arrays):
    return [pltpu.with_memory_space_constraint(a, pltpu.VMEM) for a in arrays]


def kept(*dims, dtype=F32):
    return pltpu.VMEM(dims, dtype)


def shape(*dims, dtype=F32):
    return jax.ShapeDtypeStruct(dims, dtype)


def by_head(array):
    return jnp.transpose(array, (1, 0, 2))


def to_heads(array):
    return lax.all_to_all(array, "head", split_axis=0, concat_axis=0, tiled=True)


def layer(queries, keys, values, beta, log_decay, out_gate, norm_gain):
    tokens, heads, _ = values.shape
    z = lax.axis_size("z")
    flat = lambda array: array.reshape(tokens * heads, N)
    (kv,) = call(
        pack_kernel,
        [kept(heads, tokens + 8, 2 * N, dtype=BF16)],
        [],
        remote=[flat(keys), flat(values), beta.T, log_decay.T],
        sems=10,
    )
    kv = to_heads(kv)
    qg = jnp.concatenate([by_head(queries), by_head(out_gate)], axis=2)
    blocks = kv.shape[0]
    square = kept(N, N)
    wide = kept(N, 2 * N)
    wide16 = shape(blocks, N, 2 * N, dtype=BF16)
    core = lax.axis_index("c").astype(jnp.int32).reshape(1)
    kv, qg = lax.optimization_barrier((kv, qg))
    total, en, wu_hi, wu_lo, grow, nodes = call(
        terms_kernel,
        [wide],
        near(kv),
        spill=[
            shape(blocks, N, N),
            wide16,
            wide16,
            shape(blocks, 8, N),
            shape(blocks - 1, N, 2 * N),
        ],
        sems=8,
    )
    got = lax.ppermute(total, "c", [(0, 1), (1, 0)])
    (window,) = call(pair_kernel, [square], near(total, got), core)

    def up(x, d):
        return lax.ppermute(x, "z", [(i, i + d) for i in range(z - d)])

    def cross(x, d, sources, *routes):
        pairs = [
            (2 * i + source, 2 * (i + d) + target)
            for i in sources
            for source, target in zip(routes[::2], routes[1::2])
        ]
        return lax.ppermute(x, ("z", "c"), pairs)

    span, reach_back = 1, z // 2 + 1
    while span * 2 < z:
        far = up(window, span)
        maps = lax.ppermute(window, "c", [(0, 1)])
        if span * 4 >= z:
            done = range(min(span, z - reach_back))
            fars = [cross(window, reach_back, done, 1, target) for target in (0, 1)]
        elif span * 8 >= z:
            qg, window = lax.optimization_barrier((qg, window))
            qg = to_heads(qg)
        (window,) = call(join_kernel, [square], near(window, maps, far), core)
        span *= 2
    left = range(len(done), z - reach_back)
    fars += [cross(window, reach_back, left, 1, target) for target in (0, 1)]
    own = up(window, 1)
    other = cross(window, 1, range(z - 1), 0, 1, 1, 0)
    cube = kept(blocks, N, N)
    cube16 = kept(blocks, N, N, dtype=BF16)
    r0, r1_hi, r1_lo, gate = call(
        reach_kernel,
        [cube, cube16, cube16, cube],
        [*near(kv, qg), norm_gain.reshape(1, N)],
        remote=[en, wu_hi, wu_lo, grow, nodes],
        sems=5,
    )
    (out,) = call(
        finish_kernel,
        [shape(blocks, N, N, dtype=BF16)],
        near(r0, r1_hi, r1_lo, own, other, got, gate, *fars),
        core,
    )
    return out.reshape(blocks * N, 1, N)


def solution(mesh):
    finer = Mesh(mesh.devices.reshape(-1, 2, mesh.shape["head"]), ("z", "c", "head"))
    tokens = ("z", "c", "head")
    in_specs = (
        P(tokens, None, None),
        P(tokens, None, None),
        P(tokens, None, None),
        P(tokens, None),
        P(tokens, None),
        P(tokens, None, None),
        P(),
    )
    out_specs = P(("z", "c"), "head", None)
    return jax.shard_map(layer, mesh=finer, in_specs=in_specs, out_specs=out_specs, check_vma=False)
```

profile of v0, /device:TPU:64, one launch (start us, length us, event | category | flops | bytes accessed | tf_op | source)
XLA Modules:
  0.0 94.5 jit_solution(10703853327583037171)
XLA Ops:
  0.0 3.1 %shard_map.73 = bf16[16,136,256]{2,1,0:T(8,128)(2,1)} custom-call(bf16[2048,128]{1,0:T(8,128)(2,1)} %bitcast.12, bf16[2048,128]{1,0:T(8,128)(2,1)} %bitcast.13, f32[16,128]{1,0:T(8,128)} %bitcast.14, f32[16,128]{1,0:T(8,128)} %bitcast.15), custom_call_target="tpu_custom_call" | custom-call | tf_op jit(solution)/shard_map/pallas_call | solution.py:286
  3.2 7.0 %all-to-all-start = ((bf16[16,136,256]{2,1,0:T(8,128)(2,1)}), bf16[16,136,256]{2,1,0:T(8,128)(2,1)S(1)}, u32[]{:S(2)}, u32[]{:S(2)}) async-start(bf16[16,136,256]{2,1,0:T(8,128)(2,1)} %shard_map.73), calls=%async_computation | async-start | bytes 2228224 | tf_op jit(solution)/shard_map/all_to_all | solution.py:314
  10.5 1.1 %pad_maximum_fusion = bf16[16,128,256]{2,1,0:T(8,128)(2,1)} fusion(bf16[16,128,128]{2,1,0:T(8,128)(2,1)S(1)} %get-tuple-element.33, bf16[16,128,128]{2,1,0:T(8,128)(2,1)S(1)} %get-tuple-element.34), kind=kLoop, calls=%fused_computation | loop fusion | flops 2097152 | bytes 2097152 | tf_op jit(solution)/shard_map/concatenate | solution.py:329
  11.6 17.0 %all-to-all-done.kv_ref = bf16[16,136,256]{2,1,0:T(8,128)(2,1)S(1)} async-done(((bf16[16,136,256]{2,1,0:T(8,128)(2,1)}), bf16[16,136,256]{2,1,0:T(8,128)(2,1)S(1)}, u32[]{:S(2)}, u32[]{:S(2)}) %all-to-all-start) | async-done | bytes 1114144 | tf_op jit(solution)/shard_map/all_to_all | solution.py:314
  28.7 7.1 %shard_map.74 = (f32[128,256]{1,0:T(8,128)S(1)}, f32[16,128,128]{2,1,0:T(8,128)}, bf16[16,128,256]{2,1,0:T(8,128)(2,1)}, bf16[16,128,256]{2,1,0:T(8,128)(2,1)}, ...) custom-call(bf16[16,136,256]{2,1,0:T(8,128)(2,1)S(1)} %all-to-all-done.kv_ref), custom_call_target="tpu_custom_call" | custom-call | tf_op jit(solution)/shard_map/pallas_call | solution.py:286
  35.8 1.9 %collective-permute-start = (f32[128,256]{1,0:T(8,128)S(1)}, f32[128,256]{1,0:T(8,128)S(1)}, u32[]{:S(2)}, u32[]{:S(2)}) collective-permute-start(f32[128,256]{1,0:T(8,128)S(1)} %get-tuple-element.21.own_ref), channel_id=1, source_target_pairs={{0,16},{16,0},{1,17},{17,1},{2,18},{18,2},{3,19},{19,3},{4,20},{20... | collective-permute-start | bytes 393224 | tf_op jit(solution)/shard_map/ppermute | solution.py:349
  37.7 1.3 %collective-permute-done.got_ref.first_ref = f32[128,256]{1,0:T(8,128)S(1)} collective-permute-done((f32[128,256]{1,0:T(8,128)S(1)}, f32[128,256]{1,0:T(8,128)S(1)}, u32[]{:S(2)}, u32[]{:S(2)}) %collective-permute-start) | collective-permute-done | bytes 131104 | tf_op jit(solution)/shard_map/ppermute | solution.py:349
  39.2 3.8 %collective-permute-start.2 = (f32[128,128]{1,0:T(8,128)S(1)}, f32[128,128]{1,0:T(8,128)S(1)}, u32[]{:S(2)}, u32[]{:S(2)}) collective-permute-start(f32[128,128]{1,0:T(8,128)S(1)} %shard_map.75.near_ref), channel_id=1, source_target_pairs={{0,32},{32,64},{64,96},{96,128},{128,160},{160,192},{192,224},{224... | collective-permute-start | bytes 196616 | tf_op jit(solution)/shard_map/ppermute | solution.py:353
  43.0 1.8 %collective-permute-start.1 = (f32[128,128]{1,0:T(8,128)S(1)}, f32[128,128]{1,0:T(8,128)S(1)}, u32[]{:S(2)}, u32[]{:S(2)}) collective-permute-start(f32[128,128]{1,0:T(8,128)S(1)} %shard_map.75.near_ref), channel_id=1, source_target_pairs={{0,16},{1,17},{2,18},{3,19},{4,20},{5,21},{6,22},{7,23},{8,24},{9,... | collective-permute-start | bytes 196616 | tf_op jit(solution)/shard_map/ppermute | solution.py:366
  44.8 0.5 collective-permute-done.2.far_ref
  45.9 3.7 %all-to-all-start.1 = ((bf16[16,128,256]{2,1,0:T(8,128)(2,1)}), bf16[16,128,256]{2,1,0:T(8,128)(2,1)S(1)}, u32[]{:S(2)}, u32[]{:S(2)}) async-start(bf16[16,128,256]{2,1,0:T(8,128)(2,1)} %pad_maximum_fusion), calls=%async_computation.1 | async-start | bytes 2097152 | tf_op jit(solution)/shard_map/all_to_all | solution.py:314
  49.6 7.3 %collective-permute-start.4 = (f32[128,128]{1,0:T(8,128)S(1)}, f32[128,128]{1,0:T(8,128)S(1)}, u32[]{:S(2)}, u32[]{:S(2)}) collective-permute-start(f32[128,128]{1,0:T(8,128)S(1)} %shard_map.76.near_ref), channel_id=1, source_target_pairs={{0,64},{32,96},{64,128},{96,160},{128,192},{160,224},{192,256},{22... | collective-permute-start | bytes 196616 | tf_op jit(solution)/shard_map/ppermute | solution.py:353
  56.8 1.3 %collective-permute-start.3 = (f32[128,128]{1,0:T(8,128)S(1)}, f32[128,128]{1,0:T(8,128)S(1)}, u32[]{:S(2)}, u32[]{:S(2)}) collective-permute-start(f32[128,128]{1,0:T(8,128)S(1)} %shard_map.76.near_ref), channel_id=1, source_target_pairs={{0,16},{1,17},{2,18},{3,19},{4,20},{5,21},{6,22},{7,23},{8,24},{9,... | collective-permute-start | bytes 196616 | tf_op jit(solution)/shard_map/ppermute | solution.py:366
  58.1 0.7 collective-permute-done.4.far_ref
  59.2 9.1 %collective-permute-start.6 = (f32[128,128]{1,0:T(8,128)S(1)}, f32[128,128]{1,0:T(8,128)S(1)}, u32[]{:S(2)}, u32[]{:S(2)}) collective-permute-start(f32[128,128]{1,0:T(8,128)S(1)} %shard_map.78.near_ref), channel_id=1, source_target_pairs={{0,128},{32,160},{64,192},{96,224},{128,256},{160,288},{192,320},{... | collective-permute-start | bytes 196616 | tf_op jit(solution)/shard_map/ppermute | solution.py:353
  68.3 2.0 %collective-permute-start.5 = (f32[128,128]{1,0:T(8,128)S(1)}, f32[128,128]{1,0:T(8,128)S(1)}, u32[]{:S(2)}, u32[]{:S(2)}) collective-permute-start(f32[128,128]{1,0:T(8,128)S(1)} %shard_map.78.near_ref), channel_id=1, source_target_pairs={{0,16},{1,17},{2,18},{3,19},{4,20},{5,21},{6,22},{7,23},{8,24},{9,... | collective-permute-start | bytes 196616 | tf_op jit(solution)/shard_map/ppermute | solution.py:366
  70.3 0.7 collective-permute-start.10
  70.9 0.7 collective-permute-start.9
  71.8 0.7 collective-permute-start.12
  72.5 0.7 collective-permute-start.11
  73.2 5.9 %collective-permute-start.8 = (f32[128,128]{1,0:T(8,128)S(1)}, f32[128,128]{1,0:T(8,128)S(1)}, u32[]{:S(2)}, u32[]{:S(2)}) collective-permute-start(f32[128,128]{1,0:T(8,128)S(1)} %shard_map.79), channel_id=1, source_target_pairs={{0,48},{16,32},{32,80},{48,64},{64,112},{80,96},{96,144},{112,128}... | collective-permute-start | bytes 196616 | tf_op jit(solution)/shard_map/ppermute | solution.py:361
  79.1 9.7 %collective-permute-start.7 = (f32[128,128]{1,0:T(8,128)S(1)}, f32[128,128]{1,0:T(8,128)S(1)}, u32[]{:S(2)}, u32[]{:S(2)}) collective-permute-start(f32[128,128]{1,0:T(8,128)S(1)} %shard_map.79), channel_id=1, source_target_pairs={{0,32},{32,64},{64,96},{96,128},{128,160},{160,192},{192,224},{224... | collective-permute-start | bytes 196616 | tf_op jit(solution)/shard_map/ppermute | solution.py:353
  88.8 4.0 %shard_map.77 = (f32[16,128,128]{2,1,0:T(8,128)S(1)}, bf16[16,128,128]{2,1,0:T(8,128)(2,1)S(1)}, bf16[16,128,128]{2,1,0:T(8,128)(2,1)S(1)}, f32[16,128,128]{2,1,0:T(8,128)S(1)}) custom-call(bf16[16,136,256]{2,1,0:T(8,128)(2,1)S(1)} %all-to-all-done.kv_ref, bf16[16,128,256]{2,1,0:T(8,128)(2,1)S(1)} %all-to-all-done.1.qg_ref, f32[1,128]{1,0:T(1,128)S(1)} %bitcast.11, ...), custom_call_target="tpu_custom_call" | custom-call | tf_op jit(solution)/shard_map/pallas_call | solution.py:286
  92.8 1.7 %shard_map.80 = bf16[16,128,128]{2,1,0:T(8,128)(2,1)} custom-call(s32[1]{0:T(128)} %bitcast.core_ref, f32[16,128,128]{2,1,0:T(8,128)S(1)} %get-tuple-element.28.r0_ref, bf16[16,128,128]{2,1,0:T(8,128)(2,1)S(1)} %get-tuple-element.29.hi_ref, bf16[16,128,128]{2,1,0:T(8,128)(2,1)S(1)} %get-tuple-element.30.lo_ref, ...), custom_call_target="tpu_custom_call" | custom-call | tf_op jit(solution)/shard_map/pallas_call | solution.py:286
  (22 shorter events, 1.6 us)
Async XLA Ops:
  0.0 10.2 %copy-start.1 = (bf16[128,16,128]{2,1,0:T(8,128)(2,1)S(1)}, bf16[128,16,128]{2,1,0:T(8,128)(2,1)}, u32[]{:S(2)}) copy-start(bf16[128,16,128]{2,1,0:T(8,128)(2,1)} %param.12) | copy-start | bytes 1572868
  0.0 10.2 %copy-start.2 = (bf16[128,16,128]{2,1,0:T(8,128)(2,1)S(1)}, bf16[128,16,128]{2,1,0:T(8,128)(2,1)}, u32[]{:S(2)}) copy-start(bf16[128,16,128]{2,1,0:T(8,128)(2,1)} %param.7) | copy-start | bytes 1572868
  3.2 25.5 %all-to-all-start = ((bf16[16,136,256]{2,1,0:T(8,128)(2,1)}), bf16[16,136,256]{2,1,0:T(8,128)(2,1)S(1)}, u32[]{:S(2)}, u32[]{:S(2)}) async-start(bf16[16,136,256]{2,1,0:T(8,128)(2,1)} %shard_map.73), calls=%async_computation | async-start | bytes 2228224 | tf_op jit(solution)/shard_map/all_to_all | solution.py:314
  11.6 77.2 %copy-start = (f32[128]{0:T(128)S(1)}, f32[128]{0:T(128)}, u32[]{:S(2)}) copy-start(f32[128]{0:T(128)} %param.13) | copy-start | bytes 1540
  35.8 3.2 %collective-permute-start = (f32[128,256]{1,0:T(8,128)S(1)}, f32[128,256]{1,0:T(8,128)S(1)}, u32[]{:S(2)}, u32[]{:S(2)}) collective-permute-start(f32[128,256]{1,0:T(8,128)S(1)} %get-tuple-element.21.own_ref), channel_id=1, source_target_pairs={{0,16},{16,0},{1,17},{17,1},{2,18},{18,2},{3,19},{19,3},{4,20},{20... | collective-permute-start | bytes 393224 | tf_op jit(solution)/shard_map/ppermute | solution.py:349
  39.2 6.2 %collective-permute-start.2 = (f32[128,128]{1,0:T(8,128)S(1)}, f32[128,128]{1,0:T(8,128)S(1)}, u32[]{:S(2)}, u32[]{:S(2)}) collective-permute-start(f32[128,128]{1,0:T(8,128)S(1)} %shard_map.75.near_ref), channel_id=1, source_target_pairs={{0,32},{32,64},{64,96},{96,128},{128,160},{160,192},{192,224},{224... | collective-permute-start | bytes 196616 | tf_op jit(solution)/shard_map/ppermute | solution.py:353
  43.0 2.7 %collective-permute-start.1 = (f32[128,128]{1,0:T(8,128)S(1)}, f32[128,128]{1,0:T(8,128)S(1)}, u32[]{:S(2)}, u32[]{:S(2)}) collective-permute-start(f32[128,128]{1,0:T(8,128)S(1)} %shard_map.75.near_ref), channel_id=1, source_target_pairs={{0,16},{1,17},{2,18},{3,19},{4,20},{5,21},{6,22},{7,23},{8,24},{9,... | collective-permute-start | bytes 196616 | tf_op jit(solution)/shard_map/ppermute | solution.py:366
  45.9 42.9 %all-to-all-start.1 = ((bf16[16,128,256]{2,1,0:T(8,128)(2,1)}), bf16[16,128,256]{2,1,0:T(8,128)(2,1)S(1)}, u32[]{:S(2)}, u32[]{:S(2)}) async-start(bf16[16,128,256]{2,1,0:T(8,128)(2,1)} %pad_maximum_fusion), calls=%async_computation.1 | async-start | bytes 2097152 | tf_op jit(solution)/shard_map/all_to_all | solution.py:314
  49.6 9.2 %collective-permute-start.4 = (f32[128,128]{1,0:T(8,128)S(1)}, f32[128,128]{1,0:T(8,128)S(1)}, u32[]{:S(2)}, u32[]{:S(2)}) collective-permute-start(f32[128,128]{1,0:T(8,128)S(1)} %shard_map.76.near_ref), channel_id=1, source_target_pairs={{0,64},{32,96},{64,128},{96,160},{128,192},{160,224},{192,256},{22... | collective-permute-start | bytes 196616 | tf_op jit(solution)/shard_map/ppermute | solution.py:353
  56.8 2.2 %collective-permute-start.3 = (f32[128,128]{1,0:T(8,128)S(1)}, f32[128,128]{1,0:T(8,128)S(1)}, u32[]{:S(2)}, u32[]{:S(2)}) collective-permute-start(f32[128,128]{1,0:T(8,128)S(1)} %shard_map.76.near_ref), channel_id=1, source_target_pairs={{0,16},{1,17},{2,18},{3,19},{4,20},{5,21},{6,22},{7,23},{8,24},{9,... | collective-permute-start | bytes 196616 | tf_op jit(solution)/shard_map/ppermute | solution.py:366
  59.2 12.5 %collective-permute-start.6 = (f32[128,128]{1,0:T(8,128)S(1)}, f32[128,128]{1,0:T(8,128)S(1)}, u32[]{:S(2)}, u32[]{:S(2)}) collective-permute-start(f32[128,128]{1,0:T(8,128)S(1)} %shard_map.78.near_ref), channel_id=1, source_target_pairs={{0,128},{32,160},{64,192},{96,224},{128,256},{160,288},{192,320},{... | collective-permute-start | bytes 196616 | tf_op jit(solution)/shard_map/ppermute | solution.py:353
  68.3 3.4 %collective-permute-start.5 = (f32[128,128]{1,0:T(8,128)S(1)}, f32[128,128]{1,0:T(8,128)S(1)}, u32[]{:S(2)}, u32[]{:S(2)}) collective-permute-start(f32[128,128]{1,0:T(8,128)S(1)} %shard_map.78.near_ref), channel_id=1, source_target_pairs={{0,16},{1,17},{2,18},{3,19},{4,20},{5,21},{6,22},{7,23},{8,24},{9,... | collective-permute-start | bytes 196616 | tf_op jit(solution)/shard_map/ppermute | solution.py:366
  70.3 8.8 %collective-permute-start.10 = (f32[128,128]{1,0:T(8,128)S(1)}, f32[128,128]{1,0:T(8,128)S(1)}, u32[]{:S(2)}, u32[]{:S(2)}) collective-permute-start(f32[128,128]{1,0:T(8,128)S(1)} %shard_map.78.near_ref), channel_id=1, source_target_pairs={{16,304},{48,336},{80,368},{112,400},{17,305},{49,337},{81,369},{1... | collective-permute-start | bytes 196616 | tf_op jit(solution)/shard_map/ppermute | solution.py:361
  70.9 21.8 %collective-permute-start.9 = (f32[128,128]{1,0:T(8,128)S(1)}, f32[128,128]{1,0:T(8,128)S(1)}, u32[]{:S(2)}, u32[]{:S(2)}) collective-permute-start(f32[128,128]{1,0:T(8,128)S(1)} %shard_map.78.near_ref), channel_id=1, source_target_pairs={{16,288},{48,320},{80,352},{112,384},{17,289},{49,321},{81,353},{1... | collective-permute-start | bytes 196616 | tf_op jit(solution)/shard_map/ppermute | solution.py:361
  71.8 20.9 %collective-permute-start.12 = (f32[128,128]{1,0:T(8,128)S(1)}, f32[128,128]{1,0:T(8,128)S(1)}, u32[]{:S(2)}, u32[]{:S(2)}) collective-permute-start(f32[128,128]{1,0:T(8,128)S(1)} %shard_map.79), channel_id=1, source_target_pairs={{144,432},{176,464},{208,496},{145,433},{177,465},{209,497},{146,4... | collective-permute-start | bytes 196616 | tf_op jit(solution)/shard_map/ppermute | solution.py:361
  72.5 20.3 %collective-permute-start.11 = (f32[128,128]{1,0:T(8,128)S(1)}, f32[128,128]{1,0:T(8,128)S(1)}, u32[]{:S(2)}, u32[]{:S(2)}) collective-permute-start(f32[128,128]{1,0:T(8,128)S(1)} %shard_map.79), channel_id=1, source_target_pairs={{144,416},{176,448},{208,480},{145,417},{177,449},{209,481},{146,4... | collective-permute-start | bytes 196616 | tf_op jit(solution)/shard_map/ppermute | solution.py:361
  73.2 19.6 %collective-permute-start.8 = (f32[128,128]{1,0:T(8,128)S(1)}, f32[128,128]{1,0:T(8,128)S(1)}, u32[]{:S(2)}, u32[]{:S(2)}) collective-permute-start(f32[128,128]{1,0:T(8,128)S(1)} %shard_map.79), channel_id=1, source_target_pairs={{0,48},{16,32},{32,80},{48,64},{64,112},{80,96},{96,144},{112,128}... | collective-permute-start | bytes 196616 | tf_op jit(solution)/shard_map/ppermute | solution.py:361
  79.1 13.7 %collective-permute-start.7 = (f32[128,128]{1,0:T(8,128)S(1)}, f32[128,128]{1,0:T(8,128)S(1)}, u32[]{:S(2)}, u32[]{:S(2)}) collective-permute-start(f32[128,128]{1,0:T(8,128)S(1)} %shard_map.79), channel_id=1, source_target_pairs={{0,32},{32,64},{64,96},{96,128},{128,160},{160,192},{192,224},{224... | collective-permute-start | bytes 196616 | tf_op jit(solution)/shard_map/ppermute | solution.py:353
where the time goes:
time: 95.1 us; the launch traced here: 94.5 us
  starting transfers between devices  56.1 us (59%)
  waiting for transfers between devices  20.2 us (21%)
  Pallas kernels  16.6 us (17%)
  other arithmetic  1.11 us (1%)
    ppermute x4, starting transfers between devices, up(): return lax.ppermute(x, 'z', [(i, i + d) for i in range(z - d)])  29.9 us
    all_to_all x2, waiting for transfers between devices, to_heads(): lax.all_to_all(array, 'head', split_axis=0, concat_axis=0, tiled=True)  17 us
    pallas_call x8, Pallas kernels, call(): pl.pallas_call(kernel, out_shape=[*out_shape, *(pltpu.HBM(o.shape, o.dtyp...  16.6 us
    all_to_all x2, starting transfers between devices, to_heads(): lax.all_to_all(array, 'head', split_axis=0, concat_axis=0, tiled=True)  10.7 us
    ppermute x5, starting transfers between devices, cross(): return lax.ppermute(x, ('z', 'c'), pairs)  8.55 us
    ppermute x3, starting transfers between devices, layer(): maps = lax.ppermute(window, 'c', [(0, 1)])  5.05 us
    ppermute x1, starting transfers between devices, layer(): got = lax.ppermute(total, 'c', [(0, 1), (1, 0)])  1.92 us
  transfers between devices with their start and end apart: 15, of which 7 were waited for; matrix products, arithmetic and copies ran while one was open for 1% of the time, Pallas kernels for 5%

commit v1 on v0

--- a/solution.py
+++ b/solution.py
@@ -55,7 +55,7 @@
     return lax.broadcasted_iota(jnp.int32, (N, N), 0), lax.broadcasted_iota(jnp.int32, (N, N), 1)
 
 
-def pack_kernel(k_hbm, v_hbm, beta_hbm, decay_hbm, out_ref, k_ref, v_ref, beta_ref, decay_ref, sems):
+def pack_kernel(k_hbm, v_hbm, beta_hbm, decay_hbm, out_hbm, k_ref, v_ref, beta_ref, decay_ref, out_ref, sems):
     heads, tokens = out_ref.shape[0], k_ref.shape[0] // out_ref.shape[0]
     span = N * 2 // heads
     quarter = k_ref.shape[0] // 4
@@ -70,6 +70,16 @@
     for i, (source, target) in enumerate(((beta_hbm, beta_ref), (decay_hbm, decay_ref))):
         copies.append(pltpu.make_async_copy(source, target, sems.at[8 + i]))
         copies[-1].start()
+
+    def send(first, count):
+        part = pl.ds(first, count)
+        copies.append(
+            pltpu.make_async_copy(
+                out_ref.at[:, part, :], out_hbm.at[:, part, :], sems.at[len(copies)]
+            )
+        )
+        copies[-1].start()
+
     shape2 = (2 * N, 2 * N)
     r = lax.broadcasted_iota(jnp.int32, shape2, 0)
     c = lax.broadcasted_iota(jnp.int32, shape2, 1)
@@ -82,6 +92,8 @@
         moved = dot(order, lanes(k_ref[part, :], v_ref[part, :])).astype(BF16)
         for h in range(heads):
             out_ref[h, span * i : span * (i + 1), :] = moved[span * h : span * (h + 1), :]
+        if 2 * N * (i + 1) % quarter == 0:
+            send(span * (i + 1) - tokens // 4, tokens // 4)
     copies[8].wait()
     copies[9].wait()
     both = lanes(decay_ref[...], beta_ref[...])
@@ -91,6 +103,9 @@
     for h in range(heads):
         aux = jnp.where(row == 0, high[h : h + 1, :], jnp.where(row == 1, low[h : h + 1, :], 0.0))
         out_ref[h, tokens : tokens + 8, :] = aux.astype(BF16)
+    send(tokens, 8)
+    for copy in copies[10:]:
+        copy.wait()
 
 
 def terms_kernel(kv_ref, total_ref, *rest):
@@ -320,10 +335,11 @@
     flat = lambda array: array.reshape(tokens * heads, N)
     (kv,) = call(
         pack_kernel,
-        [kept(heads, tokens + 8, 2 * N, dtype=BF16)],
+        [],
         [],
         remote=[flat(keys), flat(values), beta.T, log_decay.T],
-        sems=10,
+        spill=[shape(heads, tokens + 8, 2 * N, dtype=BF16)],
+        sems=15,
     )
     kv = to_heads(kv)
     qg = jnp.concatenate([by_head(queries), by_head(out_gate)], axis=2)

time: 95.1 us -> 94.8 us (level)
  no operation moved by 1% of the time
where the time goes in v1:
time: 94.8 us; the launch traced here: 94.3 us
  starting transfers between devices  56.1 us (59%)
  waiting for transfers between devices  20.2 us (21%)
  Pallas kernels  16.3 us (17%)
  other arithmetic  1.11 us (1%)
    ppermute x4, starting transfers between devices, up(): return lax.ppermute(x, 'z', [(i, i + d) for i in range(z - d)])  29.9 us
    all_to_all x2, waiting for transfers between devices, to_heads(): lax.all_to_all(array, 'head', split_axis=0, concat_axis=0, tiled=True)  17 us
    pallas_call x8, Pallas kernels, call(): pl.pallas_call(kernel, out_shape=[*out_shape, *(pltpu.HBM(o.shape, o.dtyp...  16.3 us
    all_to_all x2, starting transfers between devices, to_heads(): lax.all_to_all(array, 'head', split_axis=0, concat_axis=0, tiled=True)  10.7 us
    ppermute x5, starting transfers between devices, cross(): return lax.ppermute(x, ('z', 'c'), pairs)  8.56 us
    ppermute x3, starting transfers between devices, layer(): maps = lax.ppermute(window, 'c', [(0, 1)])  5.05 us
    ppermute x1, starting transfers between devices, layer(): got = lax.ppermute(total, 'c', [(0, 1), (1, 0)])  1.92 us
  transfers between devices with their start and end apart: 15, of which 7 were waited for; matrix products, arithmetic and copies ran while one was open for 1% of the time, Pallas kernels for 5%

profile of v1, /device:TPU:64, one launch (start us, length us, event | category | flops | bytes accessed | tf_op | source)
XLA Modules:
  0.0 94.3 jit_solution(12908182107389577857)
XLA Ops:
  0.0 2.9 %shard_map.73 = bf16[16,136,256]{2,1,0:T(8,128)(2,1)} custom-call(bf16[2048,128]{1,0:T(8,128)(2,1)} %bitcast.12, bf16[2048,128]{1,0:T(8,128)(2,1)} %bitcast.13, f32[16,128]{1,0:T(8,128)} %bitcast.14, f32[16,128]{1,0:T(8,128)} %bitcast.15), custom_call_target="tpu_custom_call" | custom-call | tf_op jit(solution)/shard_map/pallas_call | solution.py:301
  2.9 7.0 %all-to-all-start = ((bf16[16,136,256]{2,1,0:T(8,128)(2,1)}), bf16[16,136,256]{2,1,0:T(8,128)(2,1)S(1)}, u32[]{:S(2)}, u32[]{:S(2)}) async-start(bf16[16,136,256]{2,1,0:T(8,128)(2,1)} %shard_map.73), calls=%async_computation | async-start | bytes 2228224 | tf_op jit(solution)/shard_map/all_to_all | solution.py:329
  10.2 1.1 %pad_maximum_fusion = bf16[16,128,256]{2,1,0:T(8,128)(2,1)} fusion(bf16[16,128,128]{2,1,0:T(8,128)(2,1)S(1)} %get-tuple-element.33, bf16[16,128,128]{2,1,0:T(8,128)(2,1)S(1)} %get-tuple-element.34), kind=kLoop, calls=%fused_computation | loop fusion | flops 2097152 | bytes 2097152 | tf_op jit(solution)/shard_map/concatenate | solution.py:345
  11.4 17.0 %all-to-all-done.kv_ref = bf16[16,136,256]{2,1,0:T(8,128)(2,1)S(1)} async-done(((bf16[16,136,256]{2,1,0:T(8,128)(2,1)}), bf16[16,136,256]{2,1,0:T(8,128)(2,1)S(1)}, u32[]{:S(2)}, u32[]{:S(2)}) %all-to-all-start) | async-done | bytes 1114144 | tf_op jit(solution)/shard_map/all_to_all | solution.py:329
  28.4 7.1 %shard_map.74 = (f32[128,256]{1,0:T(8,128)S(1)}, f32[16,128,128]{2,1,0:T(8,128)}, bf16[16,128,256]{2,1,0:T(8,128)(2,1)}, bf16[16,128,256]{2,1,0:T(8,128)(2,1)}, ...) custom-call(bf16[16,136,256]{2,1,0:T(8,128)(2,1)S(1)} %all-to-all-done.kv_ref), custom_call_target="tpu_custom_call" | custom-call | tf_op jit(solution)/shard_map/pallas_call | solution.py:301
  35.5 1.9 %collective-permute-start = (f32[128,256]{1,0:T(8,128)S(1)}, f32[128,256]{1,0:T(8,128)S(1)}, u32[]{:S(2)}, u32[]{:S(2)}) collective-permute-start(f32[128,256]{1,0:T(8,128)S(1)} %get-tuple-element.21.own_ref), channel_id=1, source_target_pairs={{0,16},{16,0},{1,17},{17,1},{2,18},{18,2},{3,19},{19,3},{4,20},{20... | collective-permute-start | bytes 393224 | tf_op jit(solution)/shard_map/ppermute | solution.py:365
  37.4 1.3 %collective-permute-done.got_ref.first_ref = f32[128,256]{1,0:T(8,128)S(1)} collective-permute-done((f32[128,256]{1,0:T(8,128)S(1)}, f32[128,256]{1,0:T(8,128)S(1)}, u32[]{:S(2)}, u32[]{:S(2)}) %collective-permute-start) | collective-permute-done | bytes 131104 | tf_op jit(solution)/shard_map/ppermute | solution.py:365
  38.9 3.8 %collective-permute-start.2 = (f32[128,128]{1,0:T(8,128)S(1)}, f32[128,128]{1,0:T(8,128)S(1)}, u32[]{:S(2)}, u32[]{:S(2)}) collective-permute-start(f32[128,128]{1,0:T(8,128)S(1)} %shard_map.75.near_ref), channel_id=1, source_target_pairs={{0,32},{32,64},{64,96},{96,128},{128,160},{160,192},{192,224},{224... | collective-permute-start | bytes 196616 | tf_op jit(solution)/shard_map/ppermute | solution.py:369
  42.8 1.8 %collective-permute-start.1 = (f32[128,128]{1,0:T(8,128)S(1)}, f32[128,128]{1,0:T(8,128)S(1)}, u32[]{:S(2)}, u32[]{:S(2)}) collective-permute-start(f32[128,128]{1,0:T(8,128)S(1)} %shard_map.75.near_ref), channel_id=1, source_target_pairs={{0,16},{1,17},{2,18},{3,19},{4,20},{5,21},{6,22},{7,23},{8,24},{9,... | collective-permute-start | bytes 196616 | tf_op jit(solution)/shard_map/ppermute | solution.py:382
  44.5 0.5 collective-permute-done.2.far_ref
  45.6 3.7 %all-to-all-start.1 = ((bf16[16,128,256]{2,1,0:T(8,128)(2,1)}), bf16[16,128,256]{2,1,0:T(8,128)(2,1)S(1)}, u32[]{:S(2)}, u32[]{:S(2)}) async-start(bf16[16,128,256]{2,1,0:T(8,128)(2,1)} %pad_maximum_fusion), calls=%async_computation.1 | async-start | bytes 2097152 | tf_op jit(solution)/shard_map/all_to_all | solution.py:329
  49.3 7.3 %collective-permute-start.4 = (f32[128,128]{1,0:T(8,128)S(1)}, f32[128,128]{1,0:T(8,128)S(1)}, u32[]{:S(2)}, u32[]{:S(2)}) collective-permute-start(f32[128,128]{1,0:T(8,128)S(1)} %shard_map.76.near_ref), channel_id=1, source_target_pairs={{0,64},{32,96},{64,128},{96,160},{128,192},{160,224},{192,256},{22... | collective-permute-start | bytes 196616 | tf_op jit(solution)/shard_map/ppermute | solution.py:369
  56.6 1.3 %collective-permute-start.3 = (f32[128,128]{1,0:T(8,128)S(1)}, f32[128,128]{1,0:T(8,128)S(1)}, u32[]{:S(2)}, u32[]{:S(2)}) collective-permute-start(f32[128,128]{1,0:T(8,128)S(1)} %shard_map.76.near_ref), channel_id=1, source_target_pairs={{0,16},{1,17},{2,18},{3,19},{4,20},{5,21},{6,22},{7,23},{8,24},{9,... | collective-permute-start | bytes 196616 | tf_op jit(solution)/shard_map/ppermute | solution.py:382
  57.9 0.7 collective-permute-done.4.far_ref
  58.9 9.1 %collective-permute-start.6 = (f32[128,128]{1,0:T(8,128)S(1)}, f32[128,128]{1,0:T(8,128)S(1)}, u32[]{:S(2)}, u32[]{:S(2)}) collective-permute-start(f32[128,128]{1,0:T(8,128)S(1)} %shard_map.78.near_ref), channel_id=1, source_target_pairs={{0,128},{32,160},{64,192},{96,224},{128,256},{160,288},{192,320},{... | collective-permute-start | bytes 196616 | tf_op jit(solution)/shard_map/ppermute | solution.py:369
  68.0 2.0 %collective-permute-start.5 = (f32[128,128]{1,0:T(8,128)S(1)}, f32[128,128]{1,0:T(8,128)S(1)}, u32[]{:S(2)}, u32[]{:S(2)}) collective-permute-start(f32[128,128]{1,0:T(8,128)S(1)} %shard_map.78.near_ref), channel_id=1, source_target_pairs={{0,16},{1,17},{2,18},{3,19},{4,20},{5,21},{6,22},{7,23},{8,24},{9,... | collective-permute-start | bytes 196616 | tf_op jit(solution)/shard_map/ppermute | solution.py:382
  70.0 0.7 collective-permute-start.10
  70.7 0.7 collective-permute-start.9
  71.6 0.7 collective-permute-start.12
  72.2 0.7 collective-permute-start.11
  72.9 5.9 %collective-permute-start.8 = (f32[128,128]{1,0:T(8,128)S(1)}, f32[128,128]{1,0:T(8,128)S(1)}, u32[]{:S(2)}, u32[]{:S(2)}) collective-permute-start(f32[128,128]{1,0:T(8,128)S(1)} %shard_map.79), channel_id=1, source_target_pairs={{0,48},{16,32},{32,80},{48,64},{64,112},{80,96},{96,144},{112,128}... | collective-permute-start | bytes 196616 | tf_op jit(solution)/shard_map/ppermute | solution.py:377
  78.8 9.7 %collective-permute-start.7 = (f32[128,128]{1,0:T(8,128)S(1)}, f32[128,128]{1,0:T(8,128)S(1)}, u32[]{:S(2)}, u32[]{:S(2)}) collective-permute-start(f32[128,128]{1,0:T(8,128)S(1)} %shard_map.79), channel_id=1, source_target_pairs={{0,32},{32,64},{64,96},{96,128},{128,160},{160,192},{192,224},{224... | collective-permute-start | bytes 196616 | tf_op jit(solution)/shard_map/ppermute | solution.py:369
  88.5 3.9 %shard_map.77 = (f32[16,128,128]{2,1,0:T(8,128)S(1)}, bf16[16,128,128]{2,1,0:T(8,128)(2,1)S(1)}, bf16[16,128,128]{2,1,0:T(8,128)(2,1)S(1)}, f32[16,128,128]{2,1,0:T(8,128)S(1)}) custom-call(bf16[16,136,256]{2,1,0:T(8,128)(2,1)S(1)} %all-to-all-done.kv_ref, bf16[16,128,256]{2,1,0:T(8,128)(2,1)S(1)} %all-to-all-done.1.qg_ref, f32[1,128]{1,0:T(1,128)S(1)} %bitcast.11, ...), custom_call_target="tpu_custom_call" | custom-call | tf_op jit(solution)/shard_map/pallas_call | solution.py:301
  92.5 1.7 %shard_map.80 = bf16[16,128,128]{2,1,0:T(8,128)(2,1)} custom-call(s32[1]{0:T(128)} %bitcast.core_ref, f32[16,128,128]{2,1,0:T(8,128)S(1)} %get-tuple-element.28.r0_ref, bf16[16,128,128]{2,1,0:T(8,128)(2,1)S(1)} %get-tuple-element.29.hi_ref, bf16[16,128,128]{2,1,0:T(8,128)(2,1)S(1)} %get-tuple-element.30.lo_ref, ...), custom_call_target="tpu_custom_call" | custom-call | tf_op jit(solution)/shard_map/pallas_call | solution.py:301
  (22 shorter events, 1.6 us)
Async XLA Ops:
  0.0 9.9 %copy-start.1 = (bf16[128,16,128]{2,1,0:T(8,128)(2,1)S(1)}, bf16[128,16,128]{2,1,0:T(8,128)(2,1)}, u32[]{:S(2)}) copy-start(bf16[128,16,128]{2,1,0:T(8,128)(2,1)} %param.12) | copy-start | bytes 1572868
  0.0 9.9 %copy-start.2 = (bf16[128,16,128]{2,1,0:T(8,128)(2,1)S(1)}, bf16[128,16,128]{2,1,0:T(8,128)(2,1)}, u32[]{:S(2)}) copy-start(bf16[128,16,128]{2,1,0:T(8,128)(2,1)} %param.7) | copy-start | bytes 1572868
  2.9 25.5 %all-to-all-start = ((bf16[16,136,256]{2,1,0:T(8,128)(2,1)}), bf16[16,136,256]{2,1,0:T(8,128)(2,1)S(1)}, u32[]{:S(2)}, u32[]{:S(2)}) async-start(bf16[16,136,256]{2,1,0:T(8,128)(2,1)} %shard_map.73), calls=%async_computation | async-start | bytes 2228224 | tf_op jit(solution)/shard_map/all_to_all | solution.py:329
  11.4 77.2 %copy-start = (f32[128]{0:T(128)S(1)}, f32[128]{0:T(128)}, u32[]{:S(2)}) copy-start(f32[128]{0:T(128)} %param.13) | copy-start | bytes 1540
  35.5 3.2 %collective-permute-start = (f32[128,256]{1,0:T(8,128)S(1)}, f32[128,256]{1,0:T(8,128)S(1)}, u32[]{:S(2)}, u32[]{:S(2)}) collective-permute-start(f32[128,256]{1,0:T(8,128)S(1)} %get-tuple-element.21.own_ref), channel_id=1, source_target_pairs={{0,16},{16,0},{1,17},{17,1},{2,18},{18,2},{3,19},{19,3},{4,20},{20... | collective-permute-start | bytes 393224 | tf_op jit(solution)/shard_map/ppermute | solution.py:365
  38.9 6.2 %collective-permute-start.2 = (f32[128,128]{1,0:T(8,128)S(1)}, f32[128,128]{1,0:T(8,128)S(1)}, u32[]{:S(2)}, u32[]{:S(2)}) collective-permute-start(f32[128,128]{1,0:T(8,128)S(1)} %shard_map.75.near_ref), channel_id=1, source_target_pairs={{0,32},{32,64},{64,96},{96,128},{128,160},{160,192},{192,224},{224... | collective-permute-start | bytes 196616 | tf_op jit(solution)/shard_map/ppermute | solution.py:369
  42.8 2.7 %collective-permute-start.1 = (f32[128,128]{1,0:T(8,128)S(1)}, f32[128,128]{1,0:T(8,128)S(1)}, u32[]{:S(2)}, u32[]{:S(2)}) collective-permute-start(f32[128,128]{1,0:T(8,128)S(1)} %shard_map.75.near_ref), channel_id=1, source_target_pairs={{0,16},{1,17},{2,18},{3,19},{4,20},{5,21},{6,22},{7,23},{8,24},{9,... | collective-permute-start | bytes 196616 | tf_op jit(solution)/shard_map/ppermute | solution.py:382
  45.6 42.9 %all-to-all-start.1 = ((bf16[16,128,256]{2,1,0:T(8,128)(2,1)}), bf16[16,128,256]{2,1,0:T(8,128)(2,1)S(1)}, u32[]{:S(2)}, u32[]{:S(2)}) async-start(bf16[16,128,256]{2,1,0:T(8,128)(2,1)} %pad_maximum_fusion), calls=%async_computation.1 | async-start | bytes 2097152 | tf_op jit(solution)/shard_map/all_to_all | solution.py:329
  49.3 9.2 %collective-permute-start.4 = (f32[128,128]{1,0:T(8,128)S(1)}, f32[128,128]{1,0:T(8,128)S(1)}, u32[]{:S(2)}, u32[]{:S(2)}) collective-permute-start(f32[128,128]{1,0:T(8,128)S(1)} %shard_map.76.near_ref), channel_id=1, source_target_pairs={{0,64},{32,96},{64,128},{96,160},{128,192},{160,224},{192,256},{22... | collective-permute-start | bytes 196616 | tf_op jit(solution)/shard_map/ppermute | solution.py:369
  56.6 2.2 %collective-permute-start.3 = (f32[128,128]{1,0:T(8,128)S(1)}, f32[128,128]{1,0:T(8,128)S(1)}, u32[]{:S(2)}, u32[]{:S(2)}) collective-permute-start(f32[128,128]{1,0:T(8,128)S(1)} %shard_map.76.near_ref), channel_id=1, source_target_pairs={{0,16},{1,17},{2,18},{3,19},{4,20},{5,21},{6,22},{7,23},{8,24},{9,... | collective-permute-start | bytes 196616 | tf_op jit(solution)/shard_map/ppermute | solution.py:382
  58.9 12.5 %collective-permute-start.6 = (f32[128,128]{1,0:T(8,128)S(1)}, f32[128,128]{1,0:T(8,128)S(1)}, u32[]{:S(2)}, u32[]{:S(2)}) collective-permute-start(f32[128,128]{1,0:T(8,128)S(1)} %shard_map.78.near_ref), channel_id=1, source_target_pairs={{0,128},{32,160},{64,192},{96,224},{128,256},{160,288},{192,320},{... | collective-permute-start | bytes 196616 | tf_op jit(solution)/shard_map/ppermute | solution.py:369
  68.0 3.4 %collective-permute-start.5 = (f32[128,128]{1,0:T(8,128)S(1)}, f32[128,128]{1,0:T(8,128)S(1)}, u32[]{:S(2)}, u32[]{:S(2)}) collective-permute-start(f32[128,128]{1,0:T(8,128)S(1)} %shard_map.78.near_ref), channel_id=1, source_target_pairs={{0,16},{1,17},{2,18},{3,19},{4,20},{5,21},{6,22},{7,23},{8,24},{9,... | collective-permute-start | bytes 196616 | tf_op jit(solution)/shard_map/ppermute | solution.py:382
  70.0 8.8 %collective-permute-start.10 = (f32[128,128]{1,0:T(8,128)S(1)}, f32[128,128]{1,0:T(8,128)S(1)}, u32[]{:S(2)}, u32[]{:S(2)}) collective-permute-start(f32[128,128]{1,0:T(8,128)S(1)} %shard_map.78.near_ref), channel_id=1, source_target_pairs={{16,304},{48,336},{80,368},{112,400},{17,305},{49,337},{81,369},{1... | collective-permute-start | bytes 196616 | tf_op jit(solution)/shard_map/ppermute | solution.py:377
  70.7 21.8 %collective-permute-start.9 = (f32[128,128]{1,0:T(8,128)S(1)}, f32[128,128]{1,0:T(8,128)S(1)}, u32[]{:S(2)}, u32[]{:S(2)}) collective-permute-start(f32[128,128]{1,0:T(8,128)S(1)} %shard_map.78.near_ref), channel_id=1, source_target_pairs={{16,288},{48,320},{80,352},{112,384},{17,289},{49,321},{81,353},{1... | collective-permute-start | bytes 196616 | tf_op jit(solution)/shard_map/ppermute | solution.py:377
  71.6 20.9 %collective-permute-start.12 = (f32[128,128]{1,0:T(8,128)S(1)}, f32[128,128]{1,0:T(8,128)S(1)}, u32[]{:S(2)}, u32[]{:S(2)}) collective-permute-start(f32[128,128]{1,0:T(8,128)S(1)} %shard_map.79), channel_id=1, source_target_pairs={{144,432},{176,464},{208,496},{145,433},{177,465},{209,497},{146,4... | collective-permute-start | bytes 196616 | tf_op jit(solution)/shard_map/ppermute | solution.py:377
  72.2 20.3 %collective-permute-start.11 = (f32[128,128]{1,0:T(8,128)S(1)}, f32[128,128]{1,0:T(8,128)S(1)}, u32[]{:S(2)}, u32[]{:S(2)}) collective-permute-start(f32[128,128]{1,0:T(8,128)S(1)} %shard_map.79), channel_id=1, source_target_pairs={{144,416},{176,448},{208,480},{145,417},{177,449},{209,481},{146,4... | collective-permute-start | bytes 196616 | tf_op jit(solution)/shard_map/ppermute | solution.py:377
  72.9 19.6 %collective-permute-start.8 = (f32[128,128]{1,0:T(8,128)S(1)}, f32[128,128]{1,0:T(8,128)S(1)}, u32[]{:S(2)}, u32[]{:S(2)}) collective-permute-start(f32[128,128]{1,0:T(8,128)S(1)} %shard_map.79), channel_id=1, source_target_pairs={{0,48},{16,32},{32,80},{48,64},{64,112},{80,96},{96,144},{112,128}... | collective-permute-start | bytes 196616 | tf_op jit(solution)/shard_map/ppermute | solution.py:377
  78.8 13.7 %collective-permute-start.7 = (f32[128,128]{1,0:T(8,128)S(1)}, f32[128,128]{1,0:T(8,128)S(1)}, u32[]{:S(2)}, u32[]{:S(2)}) collective-permute-start(f32[128,128]{1,0:T(8,128)S(1)} %shard_map.79), channel_id=1, source_target_pairs={{0,32},{32,64},{64,96},{96,128},{128,160},{160,192},{192,224},{224... | collective-permute-start | bytes 196616 | tf_op jit(solution)/shard_map/ppermute | solution.py:369

commit v2 on v1

--- a/solution.py
+++ b/solution.py
@@ -175,24 +175,37 @@
         left = [square_mm(parts[b], [p * mask for p in low_parts[b]]) for b in group]
         left = [split2(x) for x in left]
         inv = [inv[b] - square_mm(left[b], parts[b]) for b in group]
-    for_u = [inv[b] * beta_row[b] for b in group]
-    for_w = [split2(for_u[b] * (grow_row[b] * nk_row[b])) for b in group]
-    for_u = [split2(x) for x in for_u]
-    w = [dot(lanes(*for_w[b]), rows(keys[b], keys[b])) for b in group]
-    values = [kv_ref[b, :N, N:] for b in group]
-    u = [dot(lanes(*for_u[b]), rows(values[b], values[b])) for b in group]
-    wu = [lanes(w[b], u[b]) for b in group]
-    for b in group:
-        wu_hi_ref[b], wu_lo_ref[b] = split2(wu[b])
-    save(1)
-    save(2)
-    last = [x[N - 1 : N, :] for x in cum]
-    tail = [jnp.exp(last[b] - cum[b]) * nk_col[b] for b in group]
-    faded = [split2(wu[b] * lanes(tail[b], tail[b])) for b in group]
-    key_t = [k.T for k in keys]
-    out = [dot(lanes(key_t[b], key_t[b]), rows(*faded[b])) for b in group]
-    pairs = [lanes(eye * jnp.exp(last[b]) - out[b][:, :N], out[b][:, N:]) for b in group]
-    spot = 0
+    pairs = [None] * blocks
+    part = blocks // 2
+    for first in range(0, blocks, part):
+        some = range(first, first + part)
+        wu = {}
+        for b in some:
+            for_u = inv[b] * beta_row[b]
+            for_w = for_u * (grow_row[b] * nk_row[b])
+            value = kv_ref[b, :N, N:]
+            w = dot(lanes(*split2(for_w)), rows(keys[b], keys[b]))
+            wu[b] = (w, dot(lanes(*split2(for_u)), rows(value, value)))
+        for b in some:
+            wu[b] = lanes(*wu[b])
+            wu_hi_ref[b], wu_lo_ref[b] = split2(wu[b])
+        save(1, first, part)
+        save(2, first, part)
+        out = {}
+        for b in some:
+            last = cum[b][N - 1 : N, :]
+            tail = jnp.exp(last - cum[b]) * nk_col[b]
+            key_t = keys[b].T
+            faded = split2(wu[b] * lanes(tail, tail))
+            out[b] = dot(lanes(key_t, key_t), rows(*faded))
+        for b in some:
+            last = jnp.exp(cum[b][N - 1 : N, :])
+            pairs[b] = lanes(eye * last - out[b][:, :N], out[b][:, N:])
+            if b % 2 == 0:
+                node_ref[b // 2] = pairs[b]
+        save(4, first // 2, part // 2)
+    spot = blocks // 2
+    pairs = [compose(pairs[i + 1], pairs[i]) for i in range(0, blocks, 2)]
     while len(pairs) > 1:
         for i in range(0, len(pairs), 2):
             node_ref[spot + i // 2] = pairs[i]
@@ -360,7 +373,7 @@
             shape(blocks, 8, N),
             shape(blocks - 1, N, 2 * N),
         ],
-        sems=8,
+        sems=11,
     )
     got = lax.ppermute(total, "c", [(0, 1), (1, 0)])
     (window,) = call(pair_kernel, [square], near(total, got), core)

time: 94.8 us -> 94.4 us (level)
  no operation moved by 1% of the time
where the time goes in v2:
time: 94.4 us; the launch traced here: 93.9 us
  starting transfers between devices  56.1 us (59%)
  waiting for transfers between devices  20.2 us (21%)
  Pallas kernels  15.9 us (17%)
  other arithmetic  1.11 us (1%)
    ppermute x4, starting transfers between devices, up(): return lax.ppermute(x, 'z', [(i, i + d) for i in range(z - d)])  29.9 us
    all_to_all x2, waiting for transfers between devices, to_heads(): lax.all_to_all(array, 'head', split_axis=0, concat_axis=0, tiled=True)  17 us
    pallas_call x8, Pallas kernels, call(): pl.pallas_call(kernel, out_shape=[*out_shape, *(pltpu.HBM(o.shape, o.dtyp...  15.9 us
    all_to_all x2, starting transfers between devices, to_heads(): lax.all_to_all(array, 'head', split_axis=0, concat_axis=0, tiled=True)  10.7 us
    ppermute x5, starting transfers between devices, cross(): return lax.ppermute(x, ('z', 'c'), pairs)  8.55 us
    ppermute x3, starting transfers between devices, layer(): maps = lax.ppermute(window, 'c', [(0, 1)])  5.05 us
    ppermute x1, starting transfers between devices, layer(): got = lax.ppermute(total, 'c', [(0, 1), (1, 0)])  1.92 us
  transfers between devices with their start and end apart: 15, of which 7 were waited for; matrix products, arithmetic and copies ran while one was open for 1% of the time, Pallas kernels for 5%

profile of v2, /device:TPU:64, one launch (start us, length us, event | category | flops | bytes accessed | tf_op | source)
XLA Modules:
  0.0 93.9 jit_solution(635020246179631047)
XLA Ops:
  0.0 2.9 %shard_map.73 = bf16[16,136,256]{2,1,0:T(8,128)(2,1)} custom-call(bf16[2048,128]{1,0:T(8,128)(2,1)} %bitcast.12, bf16[2048,128]{1,0:T(8,128)(2,1)} %bitcast.13, f32[16,128]{1,0:T(8,128)} %bitcast.14, f32[16,128]{1,0:T(8,128)} %bitcast.15), custom_call_target="tpu_custom_call" | custom-call | tf_op jit(solution)/shard_map/pallas_call | solution.py:314
  2.9 7.0 %all-to-all-start = ((bf16[16,136,256]{2,1,0:T(8,128)(2,1)}), bf16[16,136,256]{2,1,0:T(8,128)(2,1)S(1)}, u32[]{:S(2)}, u32[]{:S(2)}) async-start(bf16[16,136,256]{2,1,0:T(8,128)(2,1)} %shard_map.73), calls=%async_computation | async-start | bytes 2228224 | tf_op jit(solution)/shard_map/all_to_all | solution.py:342
  10.2 1.1 %pad_maximum_fusion = bf16[16,128,256]{2,1,0:T(8,128)(2,1)} fusion(bf16[16,128,128]{2,1,0:T(8,128)(2,1)S(1)} %get-tuple-element.33, bf16[16,128,128]{2,1,0:T(8,128)(2,1)S(1)} %get-tuple-element.34), kind=kLoop, calls=%fused_computation | loop fusion | flops 2097152 | bytes 2097152 | tf_op jit(solution)/shard_map/concatenate | solution.py:358
  11.4 17.0 %all-to-all-done.kv_ref = bf16[16,136,256]{2,1,0:T(8,128)(2,1)S(1)} async-done(((bf16[16,136,256]{2,1,0:T(8,128)(2,1)}), bf16[16,136,256]{2,1,0:T(8,128)(2,1)S(1)}, u32[]{:S(2)}, u32[]{:S(2)}) %all-to-all-start) | async-done | bytes 1114144 | tf_op jit(solution)/shard_map/all_to_all | solution.py:342
  28.4 6.7 %shard_map.74 = (f32[128,256]{1,0:T(8,128)S(1)}, f32[16,128,128]{2,1,0:T(8,128)}, bf16[16,128,256]{2,1,0:T(8,128)(2,1)}, bf16[16,128,256]{2,1,0:T(8,128)(2,1)}, ...) custom-call(bf16[16,136,256]{2,1,0:T(8,128)(2,1)S(1)} %all-to-all-done.kv_ref), custom_call_target="tpu_custom_call" | custom-call | tf_op jit(solution)/shard_map/pallas_call | solution.py:314
  35.1 1.9 %collective-permute-start = (f32[128,256]{1,0:T(8,128)S(1)}, f32[128,256]{1,0:T(8,128)S(1)}, u32[]{:S(2)}, u32[]{:S(2)}) collective-permute-start(f32[128,256]{1,0:T(8,128)S(1)} %get-tuple-element.21.own_ref), channel_id=1, source_target_pairs={{0,16},{16,0},{1,17},{17,1},{2,18},{18,2},{3,19},{19,3},{4,20},{20... | collective-permute-start | bytes 393224 | tf_op jit(solution)/shard_map/ppermute | solution.py:378
  37.1 1.3 %collective-permute-done.got_ref.first_ref = f32[128,256]{1,0:T(8,128)S(1)} collective-permute-done((f32[128,256]{1,0:T(8,128)S(1)}, f32[128,256]{1,0:T(8,128)S(1)}, u32[]{:S(2)}, u32[]{:S(2)}) %collective-permute-start) | collective-permute-done | bytes 131104 | tf_op jit(solution)/shard_map/ppermute | solution.py:378
  38.6 3.8 %collective-permute-start.2 = (f32[128,128]{1,0:T(8,128)S(1)}, f32[128,128]{1,0:T(8,128)S(1)}, u32[]{:S(2)}, u32[]{:S(2)}) collective-permute-start(f32[128,128]{1,0:T(8,128)S(1)} %shard_map.75.near_ref), channel_id=1, source_target_pairs={{0,32},{32,64},{64,96},{96,128},{128,160},{160,192},{192,224},{224... | collective-permute-start | bytes 196616 | tf_op jit(solution)/shard_map/ppermute | solution.py:382
  42.4 1.8 %collective-permute-start.1 = (f32[128,128]{1,0:T(8,128)S(1)}, f32[128,128]{1,0:T(8,128)S(1)}, u32[]{:S(2)}, u32[]{:S(2)}) collective-permute-start(f32[128,128]{1,0:T(8,128)S(1)} %shard_map.75.near_ref), channel_id=1, source_target_pairs={{0,16},{1,17},{2,18},{3,19},{4,20},{5,21},{6,22},{7,23},{8,24},{9,... | collective-permute-start | bytes 196616 | tf_op jit(solution)/shard_map/ppermute | solution.py:395
  44.2 0.5 collective-permute-done.2.far_ref
  45.2 3.7 %all-to-all-start.1 = ((bf16[16,128,256]{2,1,0:T(8,128)(2,1)}), bf16[16,128,256]{2,1,0:T(8,128)(2,1)S(1)}, u32[]{:S(2)}, u32[]{:S(2)}) async-start(bf16[16,128,256]{2,1,0:T(8,128)(2,1)} %pad_maximum_fusion), calls=%async_computation.1 | async-start | bytes 2097152 | tf_op jit(solution)/shard_map/all_to_all | solution.py:342
  48.9 7.3 %collective-permute-start.4 = (f32[128,128]{1,0:T(8,128)S(1)}, f32[128,128]{1,0:T(8,128)S(1)}, u32[]{:S(2)}, u32[]{:S(2)}) collective-permute-start(f32[128,128]{1,0:T(8,128)S(1)} %shard_map.76.near_ref), channel_id=1, source_target_pairs={{0,64},{32,96},{64,128},{96,160},{128,192},{160,224},{192,256},{22... | collective-permute-start | bytes 196616 | tf_op jit(solution)/shard_map/ppermute | solution.py:382
  56.2 1.3 %collective-permute-start.3 = (f32[128,128]{1,0:T(8,128)S(1)}, f32[128,128]{1,0:T(8,128)S(1)}, u32[]{:S(2)}, u32[]{:S(2)}) collective-permute-start(f32[128,128]{1,0:T(8,128)S(1)} %shard_map.76.near_ref), channel_id=1, source_target_pairs={{0,16},{1,17},{2,18},{3,19},{4,20},{5,21},{6,22},{7,23},{8,24},{9,... | collective-permute-start | bytes 196616 | tf_op jit(solution)/shard_map/ppermute | solution.py:395
  57.5 0.7 collective-permute-done.4.far_ref
  58.5 9.1 %collective-permute-start.6 = (f32[128,128]{1,0:T(8,128)S(1)}, f32[128,128]{1,0:T(8,128)S(1)}, u32[]{:S(2)}, u32[]{:S(2)}) collective-permute-start(f32[128,128]{1,0:T(8,128)S(1)} %shard_map.78.near_ref), channel_id=1, source_target_pairs={{0,128},{32,160},{64,192},{96,224},{128,256},{160,288},{192,320},{... | collective-permute-start | bytes 196616 | tf_op jit(solution)/shard_map/ppermute | solution.py:382
  67.6 2.0 %collective-permute-start.5 = (f32[128,128]{1,0:T(8,128)S(1)}, f32[128,128]{1,0:T(8,128)S(1)}, u32[]{:S(2)}, u32[]{:S(2)}) collective-permute-start(f32[128,128]{1,0:T(8,128)S(1)} %shard_map.78.near_ref), channel_id=1, source_target_pairs={{0,16},{1,17},{2,18},{3,19},{4,20},{5,21},{6,22},{7,23},{8,24},{9,... | collective-permute-start | bytes 196616 | tf_op jit(solution)/shard_map/ppermute | solution.py:395
  69.6 0.7 collective-permute-start.10
  70.3 0.7 collective-permute-start.9
  71.2 0.7 collective-permute-start.12
  71.9 0.7 collective-permute-start.11
  72.5 5.9 %collective-permute-start.8 = (f32[128,128]{1,0:T(8,128)S(1)}, f32[128,128]{1,0:T(8,128)S(1)}, u32[]{:S(2)}, u32[]{:S(2)}) collective-permute-start(f32[128,128]{1,0:T(8,128)S(1)} %shard_map.79), channel_id=1, source_target_pairs={{0,48},{16,32},{32,80},{48,64},{64,112},{80,96},{96,144},{112,128}... | collective-permute-start | bytes 196616 | tf_op jit(solution)/shard_map/ppermute | solution.py:390
  78.5 9.7 %collective-permute-start.7 = (f32[128,128]{1,0:T(8,128)S(1)}, f32[128,128]{1,0:T(8,128)S(1)}, u32[]{:S(2)}, u32[]{:S(2)}) collective-permute-start(f32[128,128]{1,0:T(8,128)S(1)} %shard_map.79), channel_id=1, source_target_pairs={{0,32},{32,64},{64,96},{96,128},{128,160},{160,192},{192,224},{224... | collective-permute-start | bytes 196616 | tf_op jit(solution)/shard_map/ppermute | solution.py:382
  88.2 3.9 %shard_map.77 = (f32[16,128,128]{2,1,0:T(8,128)S(1)}, bf16[16,128,128]{2,1,0:T(8,128)(2,1)S(1)}, bf16[16,128,128]{2,1,0:T(8,128)(2,1)S(1)}, f32[16,128,128]{2,1,0:T(8,128)S(1)}) custom-call(bf16[16,136,256]{2,1,0:T(8,128)(2,1)S(1)} %all-to-all-done.kv_ref, bf16[16,128,256]{2,1,0:T(8,128)(2,1)S(1)} %all-to-all-done.1.qg_ref, f32[1,128]{1,0:T(1,128)S(1)} %bitcast.11, ...), custom_call_target="tpu_custom_call" | custom-call | tf_op jit(solution)/shard_map/pallas_call | solution.py:314
  92.2 1.7 %shard_map.80 = bf16[16,128,128]{2,1,0:T(8,128)(2,1)} custom-call(s32[1]{0:T(128)} %bitcast.core_ref, f32[16,128,128]{2,1,0:T(8,128)S(1)} %get-tuple-element.28.r0_ref, bf16[16,128,128]{2,1,0:T(8,128)(2,1)S(1)} %get-tuple-element.29.hi_ref, bf16[16,128,128]{2,1,0:T(8,128)(2,1)S(1)} %get-tuple-element.30.lo_ref, ...), custom_call_target="tpu_custom_call" | custom-call | tf_op jit(solution)/shard_map/pallas_call | solution.py:314
  (22 shorter events, 1.6 us)
Async XLA Ops:
  0.0 9.9 %copy-start.1 = (bf16[128,16,128]{2,1,0:T(8,128)(2,1)S(1)}, bf16[128,16,128]{2,1,0:T(8,128)(2,1)}, u32[]{:S(2)}) copy-start(bf16[128,16,128]{2,1,0:T(8,128)(2,1)} %param.12) | copy-start | bytes 1572868
  0.0 9.9 %copy-start.2 = (bf16[128,16,128]{2,1,0:T(8,128)(2,1)S(1)}, bf16[128,16,128]{2,1,0:T(8,128)(2,1)}, u32[]{:S(2)}) copy-start(bf16[128,16,128]{2,1,0:T(8,128)(2,1)} %param.7) | copy-start | bytes 1572868
  2.9 25.5 %all-to-all-start = ((bf16[16,136,256]{2,1,0:T(8,128)(2,1)}), bf16[16,136,256]{2,1,0:T(8,128)(2,1)S(1)}, u32[]{:S(2)}, u32[]{:S(2)}) async-start(bf16[16,136,256]{2,1,0:T(8,128)(2,1)} %shard_map.73), calls=%async_computation | async-start | bytes 2228224 | tf_op jit(solution)/shard_map/all_to_all | solution.py:342
  11.4 76.8 %copy-start = (f32[128]{0:T(128)S(1)}, f32[128]{0:T(128)}, u32[]{:S(2)}) copy-start(f32[128]{0:T(128)} %param.13) | copy-start | bytes 1540
  35.1 3.2 %collective-permute-start = (f32[128,256]{1,0:T(8,128)S(1)}, f32[128,256]{1,0:T(8,128)S(1)}, u32[]{:S(2)}, u32[]{:S(2)}) collective-permute-start(f32[128,256]{1,0:T(8,128)S(1)} %get-tuple-element.21.own_ref), channel_id=1, source_target_pairs={{0,16},{16,0},{1,17},{17,1},{2,18},{18,2},{3,19},{19,3},{4,20},{20... | collective-permute-start | bytes 393224 | tf_op jit(solution)/shard_map/ppermute | solution.py:378
  38.6 6.2 %collective-permute-start.2 = (f32[128,128]{1,0:T(8,128)S(1)}, f32[128,128]{1,0:T(8,128)S(1)}, u32[]{:S(2)}, u32[]{:S(2)}) collective-permute-start(f32[128,128]{1,0:T(8,128)S(1)} %shard_map.75.near_ref), channel_id=1, source_target_pairs={{0,32},{32,64},{64,96},{96,128},{128,160},{160,192},{192,224},{224... | collective-permute-start | bytes 196616 | tf_op jit(solution)/shard_map/ppermute | solution.py:382
  42.4 2.7 %collective-permute-start.1 = (f32[128,128]{1,0:T(8,128)S(1)}, f32[128,128]{1,0:T(8,128)S(1)}, u32[]{:S(2)}, u32[]{:S(2)}) collective-permute-start(f32[128,128]{1,0:T(8,128)S(1)} %shard_map.75.near_ref), channel_id=1, source_target_pairs={{0,16},{1,17},{2,18},{3,19},{4,20},{5,21},{6,22},{7,23},{8,24},{9,... | collective-permute-start | bytes 196616 | tf_op jit(solution)/shard_map/ppermute | solution.py:395
  45.2 42.9 %all-to-all-start.1 = ((bf16[16,128,256]{2,1,0:T(8,128)(2,1)}), bf16[16,128,256]{2,1,0:T(8,128)(2,1)S(1)}, u32[]{:S(2)}, u32[]{:S(2)}) async-start(bf16[16,128,256]{2,1,0:T(8,128)(2,1)} %pad_maximum_fusion), calls=%async_computation.1 | async-start | bytes 2097152 | tf_op jit(solution)/shard_map/all_to_all | solution.py:342
  48.9 9.2 %collective-permute-start.4 = (f32[128,128]{1,0:T(8,128)S(1)}, f32[128,128]{1,0:T(8,128)S(1)}, u32[]{:S(2)}, u32[]{:S(2)}) collective-permute-start(f32[128,128]{1,0:T(8,128)S(1)} %shard_map.76.near_ref), channel_id=1, source_target_pairs={{0,64},{32,96},{64,128},{96,160},{128,192},{160,224},{192,256},{22... | collective-permute-start | bytes 196616 | tf_op jit(solution)/shard_map/ppermute | solution.py:382
  56.2 2.2 %collective-permute-start.3 = (f32[128,128]{1,0:T(8,128)S(1)}, f32[128,128]{1,0:T(8,128)S(1)}, u32[]{:S(2)}, u32[]{:S(2)}) collective-permute-start(f32[128,128]{1,0:T(8,128)S(1)} %shard_map.76.near_ref), channel_id=1, source_target_pairs={{0,16},{1,17},{2,18},{3,19},{4,20},{5,21},{6,22},{7,23},{8,24},{9,... | collective-permute-start | bytes 196616 | tf_op jit(solution)/shard_map/ppermute | solution.py:395
  58.5 12.5 %collective-permute-start.6 = (f32[128,128]{1,0:T(8,128)S(1)}, f32[128,128]{1,0:T(8,128)S(1)}, u32[]{:S(2)}, u32[]{:S(2)}) collective-permute-start(f32[128,128]{1,0:T(8,128)S(1)} %shard_map.78.near_ref), channel_id=1, source_target_pairs={{0,128},{32,160},{64,192},{96,224},{128,256},{160,288},{192,320},{... | collective-permute-start | bytes 196616 | tf_op jit(solution)/shard_map/ppermute | solution.py:382
  67.6 3.4 %collective-permute-start.5 = (f32[128,128]{1,0:T(8,128)S(1)}, f32[128,128]{1,0:T(8,128)S(1)}, u32[]{:S(2)}, u32[]{:S(2)}) collective-permute-start(f32[128,128]{1,0:T(8,128)S(1)} %shard_map.78.near_ref), channel_id=1, source_target_pairs={{0,16},{1,17},{2,18},{3,19},{4,20},{5,21},{6,22},{7,23},{8,24},{9,... | collective-permute-start | bytes 196616 | tf_op jit(solution)/shard_map/ppermute | solution.py:395
  69.6 8.8 %collective-permute-start.10 = (f32[128,128]{1,0:T(8,128)S(1)}, f32[128,128]{1,0:T(8,128)S(1)}, u32[]{:S(2)}, u32[]{:S(2)}) collective-permute-start(f32[128,128]{1,0:T(8,128)S(1)} %shard_map.78.near_ref), channel_id=1, source_target_pairs={{16,304},{48,336},{80,368},{112,400},{17,305},{49,337},{81,369},{1... | collective-permute-start | bytes 196616 | tf_op jit(solution)/shard_map/ppermute | solution.py:390
  70.3 21.8 %collective-permute-start.9 = (f32[128,128]{1,0:T(8,128)S(1)}, f32[128,128]{1,0:T(8,128)S(1)}, u32[]{:S(2)}, u32[]{:S(2)}) collective-permute-start(f32[128,128]{1,0:T(8,128)S(1)} %shard_map.78.near_ref), channel_id=1, source_target_pairs={{16,288},{48,320},{80,352},{112,384},{17,289},{49,321},{81,353},{1... | collective-permute-start | bytes 196616 | tf_op jit(solution)/shard_map/ppermute | solution.py:390
  71.2 20.9 %collective-permute-start.12 = (f32[128,128]{1,0:T(8,128)S(1)}, f32[128,128]{1,0:T(8,128)S(1)}, u32[]{:S(2)}, u32[]{:S(2)}) collective-permute-start(f32[128,128]{1,0:T(8,128)S(1)} %shard_map.79), channel_id=1, source_target_pairs={{144,432},{176,464},{208,496},{145,433},{177,465},{209,497},{146,4... | collective-permute-start | bytes 196616 | tf_op jit(solution)/shard_map/ppermute | solution.py:390
  71.9 20.3 %collective-permute-start.11 = (f32[128,128]{1,0:T(8,128)S(1)}, f32[128,128]{1,0:T(8,128)S(1)}, u32[]{:S(2)}, u32[]{:S(2)}) collective-permute-start(f32[128,128]{1,0:T(8,128)S(1)} %shard_map.79), channel_id=1, source_target_pairs={{144,416},{176,448},{208,480},{145,417},{177,449},{209,481},{146,4... | collective-permute-start | bytes 196616 | tf_op jit(solution)/shard_map/ppermute | solution.py:390
  72.5 19.6 %collective-permute-start.8 = (f32[128,128]{1,0:T(8,128)S(1)}, f32[128,128]{1,0:T(8,128)S(1)}, u32[]{:S(2)}, u32[]{:S(2)}) collective-permute-start(f32[128,128]{1,0:T(8,128)S(1)} %shard_map.79), channel_id=1, source_target_pairs={{0,48},{16,32},{32,80},{48,64},{64,112},{80,96},{96,144},{112,128}... | collective-permute-start | bytes 196616 | tf_op jit(solution)/shard_map/ppermute | solution.py:390
  78.5 13.7 %collective-permute-start.7 = (f32[128,128]{1,0:T(8,128)S(1)}, f32[128,128]{1,0:T(8,128)S(1)}, u32[]{:S(2)}, u32[]{:S(2)}) collective-permute-start(f32[128,128]{1,0:T(8,128)S(1)} %shard_map.79), channel_id=1, source_target_pairs={{0,32},{32,64},{64,96},{96,128},{128,160},{160,192},{192,224},{224... | collective-permute-start | bytes 196616 | tf_op jit(solution)/shard_map/ppermute | solution.py:382

commit v3 on v2

--- a/solution.py
+++ b/solution.py
@@ -378,33 +378,31 @@
     got = lax.ppermute(total, "c", [(0, 1), (1, 0)])
     (window,) = call(pair_kernel, [square], near(total, got), core)
 
-    def up(x, d):
-        return lax.ppermute(x, "z", [(i, i + d) for i in range(z - d)])
-
-    def cross(x, d, sources, *routes):
+    def move(x, d, *routes):
         pairs = [
             (2 * i + source, 2 * (i + d) + target)
-            for i in sources
-            for source, target in zip(routes[::2], routes[1::2])
+            for chips, source, target in routes
+            for i in chips
         ]
         return lax.ppermute(x, ("z", "c"), pairs)
 
     span, reach_back = 1, z // 2 + 1
     while span * 2 < z:
-        far = up(window, span)
-        maps = lax.ppermute(window, "c", [(0, 1)])
+        far = move(window, span, (range(span, z - span), 0, 0), (range(z - span), 1, 1))
+        maps = move(window, 0, (range(span, z), 0, 1))
         if span * 4 >= z:
             done = range(min(span, z - reach_back))
-            fars = [cross(window, reach_back, done, 1, target) for target in (0, 1)]
+            fars = [move(window, reach_back, (done, 1, target)) for target in (0, 1)]
         elif span * 8 >= z:
             qg, window = lax.optimization_barrier((qg, window))
             qg = to_heads(qg)
         (window,) = call(join_kernel, [square], near(window, maps, far), core)
         span *= 2
     left = range(len(done), z - reach_back)
-    fars += [cross(window, reach_back, left, 1, target) for target in (0, 1)]
-    own = up(window, 1)
-    other = cross(window, 1, range(z - 1), 0, 1, 1, 0)
+    fars += [move(window, reach_back, (left, 1, target)) for target in (0, 1)]
+    maps_sent = range(reach_back - 1, z - 1)
+    own = move(window, 1, (maps_sent, 0, 0), (range(z - 1), 1, 1))
+    other = move(window, 1, (maps_sent, 0, 1), (range(z - 1), 1, 0))
     cube = kept(blocks, N, N)
     cube16 = kept(blocks, N, N, dtype=BF16)
     r0, r1_hi, r1_lo, gate = call(

time: 94.4 us -> 92.2 us (0.977)
  the two profiles are of different devices: /device:TPU:64 before, /device:TPU:97 now
where the time goes in v3:
time: 92.2 us; the launch traced here: 91.6 us
  starting transfers between devices  54 us (59%)
  waiting for transfers between devices  20 us (22%)
  Pallas kernels  15.9 us (17%)
  other arithmetic  1.11 us (1%)
    ppermute x12, starting transfers between devices, move(): return lax.ppermute(x, ('z', 'c'), pairs)  39 us
    pallas_call x8, Pallas kernels, call(): pl.pallas_call(kernel, out_shape=[*out_shape, *(pltpu.HBM(o.shape, o.dtyp...  15.9 us
    all_to_all x2, waiting for transfers between devices, to_heads(): lax.all_to_all(array, 'head', split_axis=0, concat_axis=0, tiled=True)  15.3 us
    all_to_all x2, starting transfers between devices, to_heads(): lax.all_to_all(array, 'head', split_axis=0, concat_axis=0, tiled=True)  10.4 us
    ppermute x1, starting transfers between devices, layer(): got = lax.ppermute(total, 'c', [(0, 1), (1, 0)])  4.58 us
    ppermute x12, waiting for transfers between devices, move(): return lax.ppermute(x, ('z', 'c'), pairs)  3.72 us
  transfers between devices with their start and end apart: 15, of which 5 were waited for; matrix products, arithmetic and copies ran while one was open for 2% of the time, Pallas kernels for 5%

profile of v3, /device:TPU:97, one launch (start us, length us, event | category | flops | bytes accessed | tf_op | source)
XLA Modules:
  0.0 91.6 jit_solution(5910183228093695449)
XLA Ops:
  0.0 2.9 %shard_map.73 = bf16[16,136,256]{2,1,0:T(8,128)(2,1)} custom-call(bf16[2048,128]{1,0:T(8,128)(2,1)} %bitcast.12, bf16[2048,128]{1,0:T(8,128)(2,1)} %bitcast.13, f32[16,128]{1,0:T(8,128)} %bitcast.14, f32[16,128]{1,0:T(8,128)} %bitcast.15), custom_call_target="tpu_custom_call" | custom-call | tf_op jit(solution)/shard_map/pallas_call | solution.py:314
  2.9 6.8 %all-to-all-start = ((bf16[16,136,256]{2,1,0:T(8,128)(2,1)}), bf16[16,136,256]{2,1,0:T(8,128)(2,1)S(1)}, u32[]{:S(2)}, u32[]{:S(2)}) async-start(bf16[16,136,256]{2,1,0:T(8,128)(2,1)} %shard_map.73), calls=%async_computation | async-start | bytes 2228224 | tf_op jit(solution)/shard_map/all_to_all | solution.py:342
  10.0 1.1 %pad_maximum_fusion = bf16[16,128,256]{2,1,0:T(8,128)(2,1)} fusion(bf16[16,128,128]{2,1,0:T(8,128)(2,1)S(1)} %get-tuple-element.33, bf16[16,128,128]{2,1,0:T(8,128)(2,1)S(1)} %get-tuple-element.34), kind=kLoop, calls=%fused_computation | loop fusion | flops 2097152 | bytes 2097152 | tf_op jit(solution)/shard_map/concatenate | solution.py:358
  11.1 15.3 %all-to-all-done.kv_ref = bf16[16,136,256]{2,1,0:T(8,128)(2,1)S(1)} async-done(((bf16[16,136,256]{2,1,0:T(8,128)(2,1)}), bf16[16,136,256]{2,1,0:T(8,128)(2,1)S(1)}, u32[]{:S(2)}, u32[]{:S(2)}) %all-to-all-start) | async-done | bytes 1114144 | tf_op jit(solution)/shard_map/all_to_all | solution.py:342
  26.4 6.7 %shard_map.74 = (f32[128,256]{1,0:T(8,128)S(1)}, f32[16,128,128]{2,1,0:T(8,128)}, bf16[16,128,256]{2,1,0:T(8,128)(2,1)}, bf16[16,128,256]{2,1,0:T(8,128)(2,1)}, ...) custom-call(bf16[16,136,256]{2,1,0:T(8,128)(2,1)S(1)} %all-to-all-done.kv_ref), custom_call_target="tpu_custom_call" | custom-call | tf_op jit(solution)/shard_map/pallas_call | solution.py:314
  33.1 4.6 %collective-permute-start = (f32[128,256]{1,0:T(8,128)S(1)}, f32[128,256]{1,0:T(8,128)S(1)}, u32[]{:S(2)}, u32[]{:S(2)}) collective-permute-start(f32[128,256]{1,0:T(8,128)S(1)} %get-tuple-element.21.own_ref), channel_id=1, source_target_pairs={{0,16},{16,0},{1,17},{17,1},{2,18},{18,2},{3,19},{19,3},{4,20},{20... | collective-permute-start | bytes 393224 | tf_op jit(solution)/shard_map/ppermute | solution.py:378
  37.7 1.0 %collective-permute-done.got_ref.first_ref = f32[128,256]{1,0:T(8,128)S(1)} collective-permute-done((f32[128,256]{1,0:T(8,128)S(1)}, f32[128,256]{1,0:T(8,128)S(1)}, u32[]{:S(2)}, u32[]{:S(2)}) %collective-permute-start) | collective-permute-done | bytes 131104 | tf_op jit(solution)/shard_map/ppermute | solution.py:378
  38.9 4.8 %collective-permute-start.2 = (f32[128,128]{1,0:T(8,128)S(1)}, f32[128,128]{1,0:T(8,128)S(1)}, u32[]{:S(2)}, u32[]{:S(2)}) collective-permute-start(f32[128,128]{1,0:T(8,128)S(1)} %shard_map.75.near_ref), channel_id=1, source_target_pairs={{32,64},{64,96},{96,128},{128,160},{160,192},{192,224},{224,256},{... | collective-permute-start | bytes 196616 | tf_op jit(solution)/shard_map/ppermute | solution.py:387
  43.6 1.3 %collective-permute-start.1 = (f32[128,128]{1,0:T(8,128)S(1)}, f32[128,128]{1,0:T(8,128)S(1)}, u32[]{:S(2)}, u32[]{:S(2)}) collective-permute-start(f32[128,128]{1,0:T(8,128)S(1)} %shard_map.75.near_ref), channel_id=1, source_target_pairs={{32,48},{64,80},{96,112},{128,144},{160,176},{192,208},{224,240},{... | collective-permute-start | bytes 196616 | tf_op jit(solution)/shard_map/ppermute | solution.py:387
  45.0 1.8 %collective-permute-done.1.map_ref = f32[128,128]{1,0:T(8,128)S(1)} collective-permute-done((f32[128,128]{1,0:T(8,128)S(1)}, f32[128,128]{1,0:T(8,128)S(1)}, u32[]{:S(2)}, u32[]{:S(2)}) %collective-permute-start.1) | collective-permute-done | bytes 65568 | tf_op jit(solution)/shard_map/ppermute | solution.py:387
  47.0 3.7 %all-to-all-start.1 = ((bf16[16,128,256]{2,1,0:T(8,128)(2,1)}), bf16[16,128,256]{2,1,0:T(8,128)(2,1)S(1)}, u32[]{:S(2)}, u32[]{:S(2)}) async-start(bf16[16,128,256]{2,1,0:T(8,128)(2,1)} %pad_maximum_fusion), calls=%async_computation.1 | async-start | bytes 2097152 | tf_op jit(solution)/shard_map/all_to_all | solution.py:342
  50.6 4.9 %collective-permute-start.4 = (f32[128,128]{1,0:T(8,128)S(1)}, f32[128,128]{1,0:T(8,128)S(1)}, u32[]{:S(2)}, u32[]{:S(2)}) collective-permute-start(f32[128,128]{1,0:T(8,128)S(1)} %shard_map.76.near_ref), channel_id=1, source_target_pairs={{64,128},{96,160},{128,192},{160,224},{192,256},{224,288},{256,320... | collective-permute-start | bytes 196616 | tf_op jit(solution)/shard_map/ppermute | solution.py:387
  55.5 1.3 %collective-permute-start.3 = (f32[128,128]{1,0:T(8,128)S(1)}, f32[128,128]{1,0:T(8,128)S(1)}, u32[]{:S(2)}, u32[]{:S(2)}) collective-permute-start(f32[128,128]{1,0:T(8,128)S(1)} %shard_map.76.near_ref), channel_id=1, source_target_pairs={{64,80},{96,112},{128,144},{160,176},{192,208},{224,240},{256,272}... | collective-permute-start | bytes 196616 | tf_op jit(solution)/shard_map/ppermute | solution.py:387
  56.8 1.5 %collective-permute-done.4.far_ref = f32[128,128]{1,0:T(8,128)S(1)} collective-permute-done((f32[128,128]{1,0:T(8,128)S(1)}, f32[128,128]{1,0:T(8,128)S(1)}, u32[]{:S(2)}, u32[]{:S(2)}) %collective-permute-start.4) | collective-permute-done | bytes 65568 | tf_op jit(solution)/shard_map/ppermute | solution.py:387
  58.9 7.2 %collective-permute-start.6 = (f32[128,128]{1,0:T(8,128)S(1)}, f32[128,128]{1,0:T(8,128)S(1)}, u32[]{:S(2)}, u32[]{:S(2)}) collective-permute-start(f32[128,128]{1,0:T(8,128)S(1)} %shard_map.78.near_ref), channel_id=1, source_target_pairs={{128,256},{160,288},{192,320},{224,352},{256,384},{288,416},{320,4... | collective-permute-start | bytes 196616 | tf_op jit(solution)/shard_map/ppermute | solution.py:387
  66.0 0.7 collective-permute-start.5
  66.7 3.9 %collective-permute-start.10 = (f32[128,128]{1,0:T(8,128)S(1)}, f32[128,128]{1,0:T(8,128)S(1)}, u32[]{:S(2)}, u32[]{:S(2)}) collective-permute-start(f32[128,128]{1,0:T(8,128)S(1)} %shard_map.78.near_ref), channel_id=1, source_target_pairs={{16,304},{48,336},{80,368},{112,400},{17,305},{49,337},{81,369},{1... | collective-permute-start | bytes 196616 | tf_op jit(solution)/shard_map/ppermute | solution.py:387
  70.6 3.0 %collective-permute-start.9 = (f32[128,128]{1,0:T(8,128)S(1)}, f32[128,128]{1,0:T(8,128)S(1)}, u32[]{:S(2)}, u32[]{:S(2)}) collective-permute-start(f32[128,128]{1,0:T(8,128)S(1)} %shard_map.78.near_ref), channel_id=1, source_target_pairs={{16,288},{48,320},{80,352},{112,384},{17,289},{49,321},{81,353},{1... | collective-permute-start | bytes 196616 | tf_op jit(solution)/shard_map/ppermute | solution.py:387
  73.8 0.7 collective-permute-start.12
  74.5 0.7 collective-permute-start.11
  75.2 1.8 %collective-permute-start.8 = (f32[128,128]{1,0:T(8,128)S(1)}, f32[128,128]{1,0:T(8,128)S(1)}, u32[]{:S(2)}, u32[]{:S(2)}) collective-permute-start(f32[128,128]{1,0:T(8,128)S(1)} %shard_map.79), channel_id=1, source_target_pairs={{256,304},{288,336},{320,368},{352,400},{384,432},{416,464},{448,4... | collective-permute-start | bytes 196616 | tf_op jit(solution)/shard_map/ppermute | solution.py:387
  77.0 8.9 %collective-permute-start.7 = (f32[128,128]{1,0:T(8,128)S(1)}, f32[128,128]{1,0:T(8,128)S(1)}, u32[]{:S(2)}, u32[]{:S(2)}) collective-permute-start(f32[128,128]{1,0:T(8,128)S(1)} %shard_map.79), channel_id=1, source_target_pairs={{256,288},{288,320},{320,352},{352,384},{384,416},{416,448},{448,4... | collective-permute-start | bytes 196616 | tf_op jit(solution)/shard_map/ppermute | solution.py:387
  85.9 3.9 %shard_map.77 = (f32[16,128,128]{2,1,0:T(8,128)S(1)}, bf16[16,128,128]{2,1,0:T(8,128)(2,1)S(1)}, bf16[16,128,128]{2,1,0:T(8,128)(2,1)S(1)}, f32[16,128,128]{2,1,0:T(8,128)S(1)}) custom-call(bf16[16,136,256]{2,1,0:T(8,128)(2,1)S(1)} %all-to-all-done.kv_ref, bf16[16,128,256]{2,1,0:T(8,128)(2,1)S(1)} %all-to-all-done.1.qg_ref, f32[1,128]{1,0:T(1,128)S(1)} %bitcast.11, ...), custom_call_target="tpu_custom_call" | custom-call | tf_op jit(solution)/shard_map/pallas_call | solution.py:314
  89.9 1.7 %shard_map.80 = bf16[16,128,128]{2,1,0:T(8,128)(2,1)} custom-call(s32[1]{0:T(128)} %bitcast.core_ref, f32[16,128,128]{2,1,0:T(8,128)S(1)} %get-tuple-element.28.r0_ref, bf16[16,128,128]{2,1,0:T(8,128)(2,1)S(1)} %get-tuple-element.29.hi_ref, bf16[16,128,128]{2,1,0:T(8,128)(2,1)S(1)} %get-tuple-element.30.lo_ref, ...), custom_call_target="tpu_custom_call" | custom-call | tf_op jit(solution)/shard_map/pallas_call | solution.py:314
  (22 shorter events, 1.3 us)
Async XLA Ops:
  0.0 9.7 %copy-start.1 = (bf16[128,16,128]{2,1,0:T(8,128)(2,1)S(1)}, bf16[128,16,128]{2,1,0:T(8,128)(2,1)}, u32[]{:S(2)}) copy-start(bf16[128,16,128]{2,1,0:T(8,128)(2,1)} %param.12) | copy-start | bytes 1572868
  0.0 9.7 %copy-start.2 = (bf16[128,16,128]{2,1,0:T(8,128)(2,1)S(1)}, bf16[128,16,128]{2,1,0:T(8,128)(2,1)}, u32[]{:S(2)}) copy-start(bf16[128,16,128]{2,1,0:T(8,128)(2,1)} %param.7) | copy-start | bytes 1572868
  2.9 23.5 %all-to-all-start = ((bf16[16,136,256]{2,1,0:T(8,128)(2,1)}), bf16[16,136,256]{2,1,0:T(8,128)(2,1)S(1)}, u32[]{:S(2)}, u32[]{:S(2)}) async-start(bf16[16,136,256]{2,1,0:T(8,128)(2,1)} %shard_map.73), calls=%async_computation | async-start | bytes 2228224 | tf_op jit(solution)/shard_map/all_to_all | solution.py:342
  11.1 74.8 %copy-start = (f32[128]{0:T(128)S(1)}, f32[128]{0:T(128)}, u32[]{:S(2)}) copy-start(f32[128]{0:T(128)} %param.13) | copy-start | bytes 1540
  33.1 5.5 %collective-permute-start = (f32[128,256]{1,0:T(8,128)S(1)}, f32[128,256]{1,0:T(8,128)S(1)}, u32[]{:S(2)}, u32[]{:S(2)}) collective-permute-start(f32[128,256]{1,0:T(8,128)S(1)} %get-tuple-element.21.own_ref), channel_id=1, source_target_pairs={{0,16},{16,0},{1,17},{17,1},{2,18},{18,2},{3,19},{19,3},{4,20},{20... | collective-permute-start | bytes 393224 | tf_op jit(solution)/shard_map/ppermute | solution.py:378
  38.9 6.1 %collective-permute-start.2 = (f32[128,128]{1,0:T(8,128)S(1)}, f32[128,128]{1,0:T(8,128)S(1)}, u32[]{:S(2)}, u32[]{:S(2)}) collective-permute-start(f32[128,128]{1,0:T(8,128)S(1)} %shard_map.75.near_ref), channel_id=1, source_target_pairs={{32,64},{64,96},{96,128},{128,160},{160,192},{192,224},{224,256},{... | collective-permute-start | bytes 196616 | tf_op jit(solution)/shard_map/ppermute | solution.py:387
  43.6 3.1 %collective-permute-start.1 = (f32[128,128]{1,0:T(8,128)S(1)}, f32[128,128]{1,0:T(8,128)S(1)}, u32[]{:S(2)}, u32[]{:S(2)}) collective-permute-start(f32[128,128]{1,0:T(8,128)S(1)} %shard_map.75.near_ref), channel_id=1, source_target_pairs={{32,48},{64,80},{96,112},{128,144},{160,176},{192,208},{224,240},{... | collective-permute-start | bytes 196616 | tf_op jit(solution)/shard_map/ppermute | solution.py:387
  47.0 38.9 %all-to-all-start.1 = ((bf16[16,128,256]{2,1,0:T(8,128)(2,1)}), bf16[16,128,256]{2,1,0:T(8,128)(2,1)S(1)}, u32[]{:S(2)}, u32[]{:S(2)}) async-start(bf16[16,128,256]{2,1,0:T(8,128)(2,1)} %pad_maximum_fusion), calls=%async_computation.1 | async-start | bytes 2097152 | tf_op jit(solution)/shard_map/all_to_all | solution.py:342
  50.6 7.7 %collective-permute-start.4 = (f32[128,128]{1,0:T(8,128)S(1)}, f32[128,128]{1,0:T(8,128)S(1)}, u32[]{:S(2)}, u32[]{:S(2)}) collective-permute-start(f32[128,128]{1,0:T(8,128)S(1)} %shard_map.76.near_ref), channel_id=1, source_target_pairs={{64,128},{96,160},{128,192},{160,224},{192,256},{224,288},{256,320... | collective-permute-start | bytes 196616 | tf_op jit(solution)/shard_map/ppermute | solution.py:387
  55.5 3.1 %collective-permute-start.3 = (f32[128,128]{1,0:T(8,128)S(1)}, f32[128,128]{1,0:T(8,128)S(1)}, u32[]{:S(2)}, u32[]{:S(2)}) collective-permute-start(f32[128,128]{1,0:T(8,128)S(1)} %shard_map.76.near_ref), channel_id=1, source_target_pairs={{64,80},{96,112},{128,144},{160,176},{192,208},{224,240},{256,272}... | collective-permute-start | bytes 196616 | tf_op jit(solution)/shard_map/ppermute | solution.py:387
  58.9 14.8 %collective-permute-start.6 = (f32[128,128]{1,0:T(8,128)S(1)}, f32[128,128]{1,0:T(8,128)S(1)}, u32[]{:S(2)}, u32[]{:S(2)}) collective-permute-start(f32[128,128]{1,0:T(8,128)S(1)} %shard_map.78.near_ref), channel_id=1, source_target_pairs={{128,256},{160,288},{192,320},{224,352},{256,384},{288,416},{320,4... | collective-permute-start | bytes 196616 | tf_op jit(solution)/shard_map/ppermute | solution.py:387
  66.0 7.6 %collective-permute-start.5 = (f32[128,128]{1,0:T(8,128)S(1)}, f32[128,128]{1,0:T(8,128)S(1)}, u32[]{:S(2)}, u32[]{:S(2)}) collective-permute-start(f32[128,128]{1,0:T(8,128)S(1)} %shard_map.78.near_ref), channel_id=1, source_target_pairs={{128,144},{160,176},{192,208},{224,240},{256,272},{288,304},{320,3... | collective-permute-start | bytes 196616 | tf_op jit(solution)/shard_map/ppermute | solution.py:387
  66.7 10.3 %collective-permute-start.10 = (f32[128,128]{1,0:T(8,128)S(1)}, f32[128,128]{1,0:T(8,128)S(1)}, u32[]{:S(2)}, u32[]{:S(2)}) collective-permute-start(f32[128,128]{1,0:T(8,128)S(1)} %shard_map.78.near_ref), channel_id=1, source_target_pairs={{16,304},{48,336},{80,368},{112,400},{17,305},{49,337},{81,369},{1... | collective-permute-start | bytes 196616 | tf_op jit(solution)/shard_map/ppermute | solution.py:387
  70.6 19.3 %collective-permute-start.9 = (f32[128,128]{1,0:T(8,128)S(1)}, f32[128,128]{1,0:T(8,128)S(1)}, u32[]{:S(2)}, u32[]{:S(2)}) collective-permute-start(f32[128,128]{1,0:T(8,128)S(1)} %shard_map.78.near_ref), channel_id=1, source_target_pairs={{16,288},{48,320},{80,352},{112,384},{17,289},{49,321},{81,353},{1... | collective-permute-start | bytes 196616 | tf_op jit(solution)/shard_map/ppermute | solution.py:387
  73.8 16.0 %collective-permute-start.12 = (f32[128,128]{1,0:T(8,128)S(1)}, f32[128,128]{1,0:T(8,128)S(1)}, u32[]{:S(2)}, u32[]{:S(2)}) collective-permute-start(f32[128,128]{1,0:T(8,128)S(1)} %shard_map.79), channel_id=1, source_target_pairs={{144,432},{176,464},{208,496},{145,433},{177,465},{209,497},{146,4... | collective-permute-start | bytes 196616 | tf_op jit(solution)/shard_map/ppermute | solution.py:387
  74.5 15.4 %collective-permute-start.11 = (f32[128,128]{1,0:T(8,128)S(1)}, f32[128,128]{1,0:T(8,128)S(1)}, u32[]{:S(2)}, u32[]{:S(2)}) collective-permute-start(f32[128,128]{1,0:T(8,128)S(1)} %shard_map.79), channel_id=1, source_target_pairs={{144,416},{176,448},{208,480},{145,417},{177,449},{209,481},{146,4... | collective-permute-start | bytes 196616 | tf_op jit(solution)/shard_map/ppermute | solution.py:387
  75.2 14.7 %collective-permute-start.8 = (f32[128,128]{1,0:T(8,128)S(1)}, f32[128,128]{1,0:T(8,128)S(1)}, u32[]{:S(2)}, u32[]{:S(2)}) collective-permute-start(f32[128,128]{1,0:T(8,128)S(1)} %shard_map.79), channel_id=1, source_target_pairs={{256,304},{288,336},{320,368},{352,400},{384,432},{416,464},{448,4... | collective-permute-start | bytes 196616 | tf_op jit(solution)/shard_map/ppermute | solution.py:387
  77.0 12.9 %collective-permute-start.7 = (f32[128,128]{1,0:T(8,128)S(1)}, f32[128,128]{1,0:T(8,128)S(1)}, u32[]{:S(2)}, u32[]{:S(2)}) collective-permute-start(f32[128,128]{1,0:T(8,128)S(1)} %shard_map.79), channel_id=1, source_target_pairs={{256,288},{288,320},{320,352},{352,384},{384,416},{416,448},{448,4... | collective-permute-start | bytes 196616 | tf_op jit(solution)/shard_map/ppermute | solution.py:387
